TPU v7x, 128 devices: a whole 4x4x4 slice. The times are simulated.
128 devices in a mesh: dp: 8 (over z, core), tensor: 16 (over y, x).
Axes of the slice: x: 4, y: 4, z: 4, core: 2. Of those that a mesh axis runs over, the one named last changes fastest.
Arguments:
- embed_rows: bfloat16 [196608, 1024], P('tensor', 'dp'), may hold values from -6 to 6
- head_rows: bfloat16 [196608, 1024], P('tensor', 'dp'), may hold values from -6 to 6
- row_offsets: int32 [2, 17], replicated, may hold values from -2047 to 133119, as said below
- slot_table: int32 [2048], replicated, may hold values from 0 to 2047, as said below
- probe: bfloat16 [1024, 1024], replicated, may hold values from -0.1875 to 0.1875
Outputs:
- stored: bfloat16 [2048, 128, 1024], P(('dp', 'tensor'))
- sketch: float32 [2048, 128, 1024], P(('dp', 'tensor'))
Inputs may be any that keep to these rules, and one draw needn't show every extreme that they name: row_offsets[m, 16] is row_offsets[m, 0] + 131072; every entry row_offsets[m, t] with t < 16 lies strictly within 2048 rows of t * 8192, and the distance 8192 // 4 - 1 is reached above and below among ranks 1 onward in every row of every draw; row_offsets[m, 0] is never 0, above 0 for one matrix and below 0 for the other. `slot_table`: A permutation of the 2048 block numbers. Devices along dp+tensor write 16 consecutive slots each; among one device's slots exactly 1 block come from each aligned range of 8192 vocabulary rows (rows t * 8192 onward of either matrix, both matrices together).
All inputs are finite; a program needn't handle non-finite values.
Results may differ from a plain program's by a relative error of at most 0.001.
Values may be sent and summed in bfloat16 or wider, within the bound.
A program may use at most 64 MiB of HBM per device.

v0:
```python
import jax
import jax.numpy as jnp
from jax import lax
from jax.sharding import PartitionSpec as P

R = 8192
BLOCK = 128


def from_behind(block, axis, distance):
    devices = range(lax.axis_size(axis))
    route = [((i - distance) % len(devices), i) for i in devices]
    return lax.ppermute(block, axis, route)


def shards(embed_rows, head_rows, row_offsets, slot_table, probe):
    n_tensor = lax.axis_size("tensor")
    n_data = lax.axis_size("dp")
    my_tensor = lax.axis_index("tensor")
    my_data = lax.axis_index("dp")
    quarter = R // 4
    height = embed_rows.shape[0]
    col_width = embed_rows.shape[1]
    buffers = [embed_rows, head_rows]
    own_start = row_offsets[:, my_tensor]
    next_start = row_offsets[:, my_tensor + 1]
    lead_part = jnp.stack([embed_rows[:quarter], head_rows[:quarter]])
    tail_begin = jnp.clip((my_tensor + 1) * R - own_start, 0, height - quarter)
    trail_part = jnp.stack(
        [lax.dynamic_slice_in_dim(buffers[m], tail_begin[m], quarter, 0) for m in range(2)]
    )
    from_right = from_behind(lead_part, "tensor", -1)
    from_left = from_behind(trail_part, "tensor", 1)
    local_row = jnp.arange(R, dtype=jnp.int32)[:, None]
    filler = jnp.zeros((R - quarter, col_width), embed_rows.dtype)
    aligned_list = []
    for m in range(2):
        extended = jnp.concatenate([from_left[m], buffers[m], from_right[m]], axis=0)
        before = own_start[m] - my_tensor * R
        after = next_start[m] - my_tensor * R
        middle = lax.dynamic_slice_in_dim(extended, quarter - before, R, 0)
        beyond = lax.dynamic_slice_in_dim(extended, quarter + height - after, R, 0)
        leading = jnp.concatenate([from_left[m], filler], axis=0)
        aligned_list.append(
            jnp.where(local_row < before, leading, jnp.where(local_row < after, middle, beyond))
        )
    aligned = jnp.stack(aligned_list)
    blocks = aligned.reshape(2 * (R // BLOCK), BLOCK, col_width)
    devices = n_tensor * n_data
    per_rank = R // BLOCK
    total_blocks = per_rank * n_tensor
    slot_count = 2 * total_blocks // devices
    max_from = slot_count // n_tensor
    slot_grid = slot_table.reshape(devices, slot_count)
    source = slot_grid % total_blocks // per_rank
    local_block = slot_grid // total_blocks * per_rank + slot_grid % per_rank
    from_me = source == my_tensor
    rank_order = jnp.cumsum(from_me.astype(jnp.int32), axis=1) - 1
    slot_index = jnp.arange(max_from, dtype=jnp.int32)
    select = from_me[:, None, :] & (rank_order[:, None, :] == slot_index[None, :, None])
    picked = jnp.sum(jnp.where(select, local_block[:, None, :], 0), axis=2).reshape(-1)
    outgoing = blocks[picked]
    incoming = lax.all_to_all(outgoing, ("dp", "tensor"), split_axis=0, concat_axis=0, tiled=True)
    writer = my_data * n_tensor + my_tensor
    my_source = source[writer]
    slot_range = jnp.arange(slot_count, dtype=jnp.int32)
    earlier = (my_source[None, :] == my_source[:, None]) & (
        slot_range[None, :] < slot_range[:, None]
    )
    rank_within = jnp.sum(earlier.astype(jnp.int32), axis=1)
    data_range = jnp.arange(n_data, dtype=jnp.int32)
    position = (data_range[None, :] * n_tensor + my_source[:, None]) * max_from + rank_within[
        :, None
    ]
    gathered = incoming[position]
    stored = gathered.transpose(0, 2, 1, 3).reshape(slot_count, BLOCK, n_data * col_width)
    sketch = jnp.dot(
        stored.reshape(slot_count * BLOCK, n_data * col_width),
        probe,
        preferred_element_type=jnp.float32,
    ).reshape(slot_count, BLOCK, probe.shape[1])
    return (stored, sketch)


def solution(mesh):
    return jax.shard_map(
        shards,
        mesh=mesh,
        in_specs=(P("tensor", "dp"), P("tensor", "dp"), P(), P(), P()),
        out_specs=(P(("dp", "tensor"), None, None), P(("dp", "tensor"), None, None)),
        check_vma=False,
    )
```

profile of v0, /device:TPU:1, one launch (start us, length us, event | category | flops | bytes accessed | tf_op | source)
XLA Modules:
  0.0 173.2 jit_solution(7568633042060589918)
XLA Ops:
  0.7 0.9 subtract_clamp_fusion
  1.6 0.5 fusion.32
  6.0 1.8 %dynamic-slice_bitcast_fusion = (bf16[1,2048,128]{2,1,0:T(8,128)(2,1)S(1)}, bf16[1,2048,128]{2,1,0:T(8,128)(2,1)S(1)}, bf16[1,2048,128]{2,1,0:T(8,128)(2,1)S(1)}, bf16[1,2048,128]{2,1,0:T(8,128)(2,1)S(1)}) fusion(bf16[12288,128]{1,0:T(8,128)(2,1)} %param.6, s32[]{:T(128)S(6)} %select_n.131, bf16[12288,128]{1,0:T(8,128)(2,1)} %param.5, s32[]{:T(128)S(6)} %select_n.130), kind=kLoop, calls=%fused_computation.21 | loop fusion | bytes 4194312 | tf_op jit(solution)/shard_map/stack | solution.py:29
  7.8 1.1 pad_maximum_fusion.4
  8.9 5.7 %collective-permute-start.1 = (bf16[2,2048,128]{2,1,0:T(8,128)(2,1)}, bf16[2,2048,128]{2,1,0:T(8,128)(2,1)S(1)}, u32[]{:S(2)}, u32[]{:S(2)}) collective-permute-start(bf16[2,2048,128]{2,1,0:T(8,128)(2,1)} %pad_maximum_fusion.4), channel_id=1, source_target_pairs={{1,0},{2,1},{3,2},{4,3},{5,4},{6,5},{7,6},{8,7},{9,8},{10,9},{11,1... | collective-permute-start | bytes 3145736 | tf_op jit(solution)/shard_map/ppermute | solution.py:13
  14.6 1.1 pad_maximum_fusion.3
  15.7 0.6 fusion.30
  18.9 0.2 fusion.33
  19.2 17.6 %collective-permute-done.1 = bf16[2,2048,128]{2,1,0:T(8,128)(2,1)S(1)} collective-permute-done((bf16[2,2048,128]{2,1,0:T(8,128)(2,1)}, bf16[2,2048,128]{2,1,0:T(8,128)(2,1)S(1)}, u32[]{:S(2)}, u32[]{:S(2)}) %collective-permute-start.1) | collective-permute-done | bytes 1048608 | tf_op jit(solution)/shard_map/ppermute | solution.py:13
  36.8 6.2 %collective-permute-done = bf16[2,2048,128]{2,1,0:T(8,128)(2,1)} collective-permute-done((bf16[2,2048,128]{2,1,0:T(8,128)(2,1)}, bf16[2,2048,128]{2,1,0:T(8,128)(2,1)}, u32[]{:S(2)}, u32[]{:S(2)}) %collective-permute-start) | collective-permute-done | bytes 1048608 | tf_op jit(solution)/shard_map/ppermute | solution.py:13
  43.1 1.3 slice_bitcast_fusion.3
  44.4 13.4 %pad_maximum_fusion = bf16[16384,128]{1,0:T(8,128)(2,1)S(1)} fusion(bf16[2048,128]{1,0:T(8,128)(2,1)S(1)} %get-tuple-element.16, bf16[12288,128]{1,0:T(8,128)(2,1)S(1)} %copy-done.1, bf16[2048,128]{1,0:T(8,128)(2,1)S(1)} %get-tuple-element.14), kind=kLoop, calls=%fused_computation.2 | loop fusion | flops 12582912 | bytes 8388608 | tf_op jit(solution)/shard_map/concatenate | solution.py:38
  57.8 13.6 %pad_maximum_fusion.1 = bf16[16384,128]{1,0:T(8,128)(2,1)S(1)} fusion(bf16[2048,128]{1,0:T(8,128)(2,1)S(1)} %get-tuple-element.17, bf16[12288,128]{1,0:T(8,128)(2,1)S(1)} %copy-done.2, bf16[2048,128]{1,0:T(8,128)(2,1)S(1)} %get-tuple-element.15), kind=kLoop, calls=%fused_computation.3 | loop fusion | flops 12582912 | bytes 8388608 | tf_op jit(solution)/shard_map/concatenate | solution.py:38
  71.4 4.2 %select_bitcast_fusion.1 = bf16[1,8192,128]{2,1,0:T(8,128)(2,1)S(1)} fusion(bf16[16384,128]{1,0:T(8,128)(2,1)S(1)} %pad_maximum_fusion, s32[]{:T(128)S(6)} %select_n.134, s32[]{:T(128)S(6)} %select_n.133, bf16[2048,128]{1,0:T(8,128)(2,1)S(1)} %get-tuple-element.14, pred[8192]{0:T(1024)(128)(4,1)S(1)} %iota_compare_fusion.2, ...), kind=kLoop, calls=%fused_computation.8 | loop fusion | flops 2097152 | bytes 6832136 | tf_op jit(solution)/shard_map/stack | solution.py:47
  75.6 4.2 %select_bitcast_fusion = bf16[1,8192,128]{2,1,0:T(8,128)(2,1)S(1)} fusion(bf16[16384,128]{1,0:T(8,128)(2,1)S(1)} %pad_maximum_fusion.1, s32[]{:T(128)S(6)} %select_n.138, s32[]{:T(128)S(6)} %select_n.137, bf16[2048,128]{1,0:T(8,128)(2,1)S(1)} %get-tuple-element.15, pred[8192]{0:T(1024)(128)(4,1)S(1)} %iota_compare_fusion, ...), kind=kLoop, calls=%fused_computation.7 | loop fusion | flops 2097152 | bytes 6832136 | tf_op jit(solution)/shard_map/stack | solution.py:47
  79.9 2.4 %pad_maximum_fusion.2 = bf16[2,8192,128]{2,1,0:T(8,128)(2,1)} fusion(bf16[1,8192,128]{2,1,0:T(8,128)(2,1)S(1)} %select_bitcast_fusion, bf16[1,8192,128]{2,1,0:T(8,128)(2,1)S(1)} %select_bitcast_fusion.1), kind=kLoop, calls=%fused_computation.4 | loop fusion | flops 2097152 | bytes 8388608 | tf_op jit(solution)/shard_map/stack | solution.py:47
  82.2 5.3 %gather_fusion = bf16[128,128,128]{2,1,0:T(8,128)(2,1)} fusion(bf16[128,128,128]{2,1,0:T(8,128)(2,1)} %bitcast.44, s32[1024]{0:T(1024)S(1)} %pad_clamp_fusion.1), kind=kCustom, calls=%fused_computation | custom fusion | bytes 8389120 | tf_op jit(solution)/shard_map/gather | solution.py:62
  87.5 7.2 %all-to-all-start = ((bf16[128,128,128]{2,1,0:T(8,128)(2,1)}), bf16[128,128,128]{2,1,0:T(8,128)(2,1)}, u32[]{:S(2)}, u32[]{:S(2)}) async-start(bf16[128,128,128]{2,1,0:T(8,128)(2,1)} %gather_fusion), calls=%async_computation | async-start | bytes 8388608 | tf_op jit(solution)/shard_map/all_to_all | solution.py:63
  94.9 0.2 convert_reduce_fusion
  95.3 50.9 %all-to-all-done = bf16[128,128,128]{2,1,0:T(8,128)(2,1)} async-done(((bf16[128,128,128]{2,1,0:T(8,128)(2,1)}), bf16[128,128,128]{2,1,0:T(8,128)(2,1)}, u32[]{:S(2)}, u32[]{:S(2)}) %all-to-all-start) | async-done | bytes 4194336 | tf_op jit(solution)/shard_map/all_to_all | solution.py:63
  146.2 5.3 %gather_fusion.1 = bf16[128,128,128]{2,1,0:T(8,128)(2,1)} fusion(bf16[128,128,128]{2,1,0:T(8,128)(2,1)} %all-to-all-done, s32[1024]{0:T(1024)S(1)} %pad_clamp_fusion), kind=kCustom, calls=%fused_computation.1 | custom fusion | bytes 8389120 | tf_op jit(solution)/shard_map/gather | solution.py:75
  151.5 6.4 %copy.22 = bf16[16,128,8,128]{1,3,2,0:T(8,128)(2,1)} copy(bf16[16,128,8,128]{3,1,2,0:T(8,128)(2,1)} %bitcast.43) | data formatting | bytes 8388608 | tf_op jit(solution)/shard_map/transpose | solution.py:76
  157.9 6.4 %copy.24 = bf16[16,128,1024]{2,1,0:T(8,128)(2,1)} copy(bf16[16,128,1024]{1,2,0:T(8,128)(2,1)} %bitcast.45) | data formatting | bytes 8388608
  164.3 9.0 %fusion = f32[16,128,1024]{2,1,0:T(8,128)} fusion(bf16[16,128,1024]{1,2,0:T(8,128)(2,1)} %bitcast.46, bf16[1024,1024]{1,0:T(8,128)(2,1)S(1)} %copy-done), kind=kOutput, calls=%fused_computation.5 | convolution fusion | flops 4294967296 | bytes 14680064 | tf_op jit(solution)/shard_map/dot_general | solution.py:77
  (26 shorter events, 0.6 us)
Async XLA Ops:
  0.6 163.6 %copy-start = (bf16[1024,1024]{1,0:T(8,128)(2,1)S(1)}, bf16[1024,1024]{1,0:T(8,128)(2,1)}, u32[]{:S(2)}) copy-start(bf16[1024,1024]{1,0:T(8,128)(2,1)} %param.9) | copy-start | bytes 6291460
  6.0 12.8 %copy-start.3 = (s32[2048]{0:T(1024)S(1)}, s32[2048]{0:T(1024)}, u32[]{:S(2)}) copy-start(s32[2048]{0:T(1024)} %param.8) | copy-start | bytes 24580
  8.9 27.9 %collective-permute-start.1 = (bf16[2,2048,128]{2,1,0:T(8,128)(2,1)}, bf16[2,2048,128]{2,1,0:T(8,128)(2,1)S(1)}, u32[]{:S(2)}, u32[]{:S(2)}) collective-permute-start(bf16[2,2048,128]{2,1,0:T(8,128)(2,1)} %pad_maximum_fusion.4), channel_id=1, source_target_pairs={{1,0},{2,1},{3,2},{4,3},{5,4},{6,5},{7,6},{8,7},{9,8},{10,9},{11,1... | collective-permute-start | bytes 3145736 | tf_op jit(solution)/shard_map/ppermute | solution.py:13
  15.7 27.4 %collective-permute-start = (bf16[2,2048,128]{2,1,0:T(8,128)(2,1)}, bf16[2,2048,128]{2,1,0:T(8,128)(2,1)}, u32[]{:S(2)}, u32[]{:S(2)}) collective-permute-start(bf16[2,2048,128]{2,1,0:T(8,128)(2,1)} %pad_maximum_fusion.3), channel_id=1, source_target_pairs={{15,0},{0,1},{1,2},{2,3},{3,4},{4,5},{5,6},{6,7},{7,8},{8,9},{9,10... | collective-permute-start | bytes 3145736 | tf_op jit(solution)/shard_map/ppermute | solution.py:13
  18.9 25.4 %copy-start.1 = (bf16[12288,128]{1,0:T(8,128)(2,1)S(1)}, bf16[12288,128]{1,0:T(8,128)(2,1)}, u32[]{:S(2)}) copy-start(bf16[12288,128]{1,0:T(8,128)(2,1)} %param.5) | copy-start | bytes 9437188
  44.4 13.4 %copy-start.2 = (bf16[12288,128]{1,0:T(8,128)(2,1)S(1)}, bf16[12288,128]{1,0:T(8,128)(2,1)}, u32[]{:S(2)}) copy-start(bf16[12288,128]{1,0:T(8,128)(2,1)} %param.6) | copy-start | bytes 9437188
  87.5 58.7 %all-to-all-start = ((bf16[128,128,128]{2,1,0:T(8,128)(2,1)}), bf16[128,128,128]{2,1,0:T(8,128)(2,1)}, u32[]{:S(2)}, u32[]{:S(2)}) async-start(bf16[128,128,128]{2,1,0:T(8,128)(2,1)} %gather_fusion), calls=%async_computation | async-start | bytes 8388608 | tf_op jit(solution)/shard_map/all_to_all | solution.py:63
where the time goes:
time: 174 us; the launch traced here: 173 us
  waiting for transfers between devices  74.7 us (43%)
  other arithmetic  41.5 us (24%)
  local copies, waits for them, and re-layouts  27.9 us (16%)
  starting transfers between devices  12.9 us (7%)
  matrix products  8.97 us (5%)
  between operations  7.25 us (4%)
    all_to_all x1, waiting for transfers between devices, shards(): lax.all_to_all(outgoing, ('dp', 'tensor'), split_axis=0, concat_axis=0, t...  50.9 us
    concatenate x2, other arithmetic, shards(): jnp.concatenate([from_left[m], buffers[m], from_right[m]], axis=0)  27 us
    ppermute x2, waiting for transfers between devices, from_behind(): return lax.ppermute(block, axis, route)  23.8 us
    another operation x3, other arithmetic, shards(): aligned = jnp.stack(aligned_list)  10.8 us
    dot_general x1, matrix products, shards(): jnp.dot(stored.reshape(slot_count * BLOCK, n_data * col_width), probe, pr...  8.97 us
    all_to_all x1, starting transfers between devices, shards(): lax.all_to_all(outgoing, ('dp', 'tensor'), split_axis=0, concat_axis=0, t...  7.18 us
    unnamed x9, local copies, waits for them, and re-layouts  6.42 us
    transpose x1, local copies, waits for them, and re-layouts, shards(): gathered.transpose(0, 2, 1, 3)  6.39 us
  transfers between devices with their start and end apart: 3, of which 3 were waited for; matrix products, arithmetic and copies ran while one was open for 1% of the time, Pallas kernels for 0%

commit v1 on v0

v1 whole, which is shorter than its diff:
```python
import functools

import jax
import jax.numpy as jnp
from jax import lax
from jax.experimental import pallas as pl
from jax.experimental.pallas import tpu as pltpu
from jax.sharding import PartitionSpec as P

R = 8192
BLOCK = 128
GROUP = 8


def from_behind(block, axis, distance):
    devices = range(lax.axis_size(axis))
    route = [((i - distance) % len(devices), i) for i in devices]
    return lax.ppermute(block, axis, route)


def own_kernel(quarter, before, dest, embed, head, out, ext, wide, packed, load_sem, store_sem):
    rows = GROUP * BLOCK
    groups = R // rows
    chunks = (R + quarter) // rows
    per_rank = R // BLOCK
    for m, source in enumerate((embed, head)):
        for c in range(chunks):
            pltpu.make_async_copy(
                source.at[pl.ds(c * rows, rows)],
                ext.at[m, pl.ds(quarter + c * rows, rows)],
                load_sem.at[m, c],
            ).start()
    ahead = quarter // rows
    for m, source in enumerate((embed, head)):
        for g in range(groups):
            for c in range(chunks):
                if c == g + ahead or (g == 0 and c < ahead):
                    pltpu.make_async_copy(
                        source.at[pl.ds(c * rows, rows)],
                        ext.at[m, pl.ds(quarter + c * rows, rows)],
                        load_sem.at[m, c],
                    ).wait()
            start = quarter + g * rows - before[m]
            aligned = start // 16 * 16
            offset = start - aligned
            slot = g % 2
            wide[slot] = ext[m, pl.ds(pl.multiple_of(aligned, 16), rows + 16), :].astype(jnp.float32)
            first = m * per_rank + g * GROUP
            packed[pl.ds(first * BLOCK, rows), :] = wide[slot, pl.ds(offset, rows), :].astype(jnp.bfloat16)
            for b in range(GROUP):
                block = first + b
                pltpu.make_async_copy(
                    packed.at[pl.ds(block * BLOCK, BLOCK)], out.at[dest[block]], store_sem.at[block]
                ).start()

    @pl.loop(0, 2 * per_rank)
    def _(block):
        pltpu.make_async_copy(
            packed.at[pl.ds(0, BLOCK)], out.at[dest[block]], store_sem.at[block]
        ).wait()


def pack_own(embed_rows, head_rows, before, dest, quarter):
    blocks = 2 * (R // BLOCK)
    rows = GROUP * BLOCK
    width = embed_rows.shape[1]
    chunks = (R + quarter) // rows
    return pl.pallas_call(
        functools.partial(own_kernel, quarter),
        grid_spec=pltpu.PrefetchScalarGridSpec(
            num_scalar_prefetch=2,
            grid=(),
            in_specs=[pl.BlockSpec(memory_space=pl.ANY)] * 2,
            out_specs=pl.BlockSpec(memory_space=pl.ANY),
            scratch_shapes=[
                pltpu.VMEM((2, R + 2 * quarter + rows, width), jnp.bfloat16),
                pltpu.VMEM((2, rows + 16, width), jnp.float32),
                pltpu.VMEM((blocks * BLOCK, width), jnp.bfloat16),
                pltpu.SemaphoreType.DMA((2, chunks)),
                pltpu.SemaphoreType.DMA((blocks,)),
            ],
        ),
        out_shape=jax.ShapeDtypeStruct((blocks, BLOCK, width), embed_rows.dtype),
        cost_estimate=pl.CostEstimate(flops=0, bytes_accessed=10 << 20, transcendentals=0),
    )(before, dest, embed_rows, head_rows)


def patch_kernel(quarter, before, after, dest, left, right, _, out, lbuf, rbuf, wide, edge, packed,
                 load_sem, edge_sem, store_sem):
    per_rank = R // BLOCK
    most = quarter // BLOCK + 1
    lead = BLOCK

    def load_left(m):
        return pltpu.make_async_copy(left.at[m], lbuf.at[m], load_sem.at[0, m])

    def load_right(m):
        return pltpu.make_async_copy(right.at[m], rbuf.at[m], load_sem.at[1, m])

    def load_edge(side, m, block):
        return pltpu.make_async_copy(out.at[dest[block]], edge.at[side, m], edge_sem.at[side, m])

    def store(side, m, i, block):
        return pltpu.make_async_copy(
            packed.at[side, m, i], out.at[dest[block]], store_sem.at[side, m, i]
        )

    row = lax.broadcasted_iota(jnp.int32, (BLOCK, lbuf.shape[-1]), 0)
    counts = []
    for m in range(2):
        n_left = (jnp.maximum(before[m], 0) + BLOCK - 1) // BLOCK
        first = jnp.minimum(after[m] // BLOCK, per_rank)
        n_right = per_rank - first
        counts.append((n_left, first, n_right))

        @pl.when(n_left > 0)
        def _():
            load_left(m).start()
            load_edge(0, m, m * per_rank + n_left - 1).start()

        @pl.when(n_right > 0)
        def _():
            load_right(m).start()
            load_edge(1, m, m * per_rank + first).start()

    for m in range(2):
        n_left, first, n_right = counts[m]

        @pl.when(n_left > 0)
        def _():
            load_left(m).wait()
            load_edge(0, m, m * per_rank + n_left - 1).wait()

            @pl.loop(0, n_left)
            def _(i):
                x = lbuf[m, pl.ds(pl.multiple_of(i * BLOCK, BLOCK), BLOCK), :].astype(jnp.float32)
                keep = edge[0, m].astype(jnp.float32)
                x = jnp.where(row + i * BLOCK < before[m], x, keep)
                packed[0, m, i] = x.astype(jnp.bfloat16)
                store(0, m, i, m * per_rank + i).start()

        @pl.when(n_right > 0)
        def _():
            load_right(m).wait()
            load_edge(1, m, m * per_rank + first).wait()
            wide[m, pl.ds(lead, quarter), :] = rbuf[m].astype(jnp.float32)
            skip = after[m] - first * BLOCK

            @pl.loop(0, n_right)
            def _(i):
                x = wide[m, pl.ds(lead + i * BLOCK - skip, BLOCK), :]
                keep = edge[1, m].astype(jnp.float32)
                x = jnp.where(row + i * BLOCK >= skip, x, keep)
                packed[1, m, i] = x.astype(jnp.bfloat16)
                store(1, m, i, m * per_rank + first + i).start()

    for m in range(2):
        n_left, first, n_right = counts[m]

        @pl.loop(0, n_left)
        def _(i):
            store(0, m, i, m * per_rank + i).wait()

        @pl.loop(0, n_right)
        def _(i):
            store(1, m, i, m * per_rank + first + i).wait()


def patch(outgoing, left, right, before, after, dest):
    quarter, width = left.shape[1:]
    most = quarter // BLOCK + 1
    dtype = outgoing.dtype
    return pl.pallas_call(
        functools.partial(patch_kernel, quarter),
        grid_spec=pltpu.PrefetchScalarGridSpec(
            num_scalar_prefetch=3,
            grid=(),
            in_specs=[pl.BlockSpec(memory_space=pl.ANY)] * 3,
            out_specs=pl.BlockSpec(memory_space=pl.ANY),
            scratch_shapes=[
                pltpu.VMEM((2, quarter, width), dtype),
                pltpu.VMEM((2, quarter, width), dtype),
                pltpu.VMEM((2, quarter + 2 * BLOCK, width), jnp.float32),
                pltpu.VMEM((2, 2, BLOCK, width), dtype),
                pltpu.VMEM((2, 2, most, BLOCK, width), dtype),
                pltpu.SemaphoreType.DMA((2, 2)),
                pltpu.SemaphoreType.DMA((2, 2)),
                pltpu.SemaphoreType.DMA((2, 2, most)),
            ],
        ),
        out_shape=jax.ShapeDtypeStruct(outgoing.shape, dtype),
        input_output_aliases={5: 0},
        cost_estimate=pl.CostEstimate(flops=0, bytes_accessed=6 << 20, transcendentals=0),
    )(before, after, dest, left, right, outgoing)


PAIR = 2


def finish_kernel(source, *refs):
    pieces = refs[:PAIR]
    probe, stored, sketch = refs[PAIR:]
    n_data, height, width = pieces[0].shape
    for i in range(PAIR):
        for d in range(n_data):
            stored[i, :, d * width:(d + 1) * width] = pieces[i][d]
    x = stored[...].reshape(PAIR * height, n_data * width)
    y = jnp.dot(x, probe[...], preferred_element_type=jnp.float32)
    sketch[...] = y.reshape(sketch.shape)


def finish(incoming, probe, source):
    n_data, n_tensor, height, width = incoming.shape
    slots = source.shape[0]
    columns = n_data * width

    def piece(i):
        return pl.BlockSpec(
            (n_data, None, height, width), lambda g, source: (0, source[g * PAIR + i], 0, 0)
        )

    return pl.pallas_call(
        finish_kernel,
        grid_spec=pltpu.PrefetchScalarGridSpec(
            num_scalar_prefetch=1,
            grid=(slots // PAIR,),
            in_specs=[piece(i) for i in range(PAIR)]
            + [pl.BlockSpec(probe.shape, lambda g, source: (0, 0))],
            out_specs=[
                pl.BlockSpec((PAIR, height, columns), lambda g, source: (g, 0, 0)),
                pl.BlockSpec((PAIR, height, probe.shape[1]), lambda g, source: (g, 0, 0)),
            ],
        ),
        out_shape=[
            jax.ShapeDtypeStruct((slots, height, columns), incoming.dtype),
            jax.ShapeDtypeStruct((slots, height, probe.shape[1]), jnp.float32),
        ],
        cost_estimate=pl.CostEstimate(
            flops=2 * slots * height * columns * probe.shape[1],
            bytes_accessed=18 << 20,
            transcendentals=0,
        ),
    )(source, *([incoming] * PAIR), probe)


def shards(embed_rows, head_rows, row_offsets, slot_table, probe):
    n_tensor = lax.axis_size("tensor")
    n_data = lax.axis_size("dp")
    my_tensor = lax.axis_index("tensor")
    my_data = lax.axis_index("dp")
    quarter = R // 4
    height, width = embed_rows.shape
    buffers = [embed_rows, head_rows]
    own_start = row_offsets[:, my_tensor]
    next_start = row_offsets[:, my_tensor + 1]
    before = own_start - my_tensor * R
    after = next_start - my_tensor * R
    lead_part = jnp.stack([embed_rows[:quarter], head_rows[:quarter]])
    tail_begin = jnp.clip((my_tensor + 1) * R - own_start, 0, height - quarter)
    trail_part = jnp.stack(
        [lax.dynamic_slice_in_dim(buffers[m], tail_begin[m], quarter, 0) for m in range(2)]
    )
    from_right = from_behind(lead_part, "tensor", -1)
    from_left = from_behind(trail_part, "tensor", 1)

    devices = n_tensor * n_data
    per_rank = R // BLOCK
    total_blocks = per_rank * n_tensor
    slot_count = 2 * total_blocks // devices
    local = jnp.arange(2 * per_rank, dtype=jnp.int32)
    number = local // per_rank * total_blocks + my_tensor * per_rank + local % per_rank
    holder = jnp.arange(2 * total_blocks, dtype=jnp.int32) // slot_count
    dest = jnp.sum(jnp.where(slot_table[None, :] == number[:, None], holder[None, :], 0), axis=1)
    dest = dest.astype(jnp.int32)

    outgoing = pack_own(embed_rows, head_rows, before, dest, quarter)
    outgoing = patch(outgoing, from_left, from_right, before, after, dest)
    incoming = lax.all_to_all(outgoing, ("dp", "tensor"), split_axis=0, concat_axis=0, tiled=True)
    writer = my_data * n_tensor + my_tensor
    mine = lax.dynamic_slice_in_dim(slot_table, writer * slot_count, slot_count)
    source = mine % total_blocks // per_rank
    incoming = incoming.reshape(n_data, n_tensor, BLOCK, width)
    stored, sketch = finish(incoming, probe, source)
    return (stored, sketch)


def solution(mesh):
    return jax.shard_map(
        shards,
        mesh=mesh,
        in_specs=(P("tensor", "dp"), P("tensor", "dp"), P(), P(), P()),
        out_specs=(P(("dp", "tensor"), None, None), P(("dp", "tensor"), None, None)),
        check_vma=False,
    )
```

time: 174 us -> 116 us (0.67)
  other arithmetic: 41.5 us -> 3.18 us
  local copies, waits for them, and re-layouts: 27.9 us -> 3.29 us
  Pallas kernels: 0 us -> 21 us
  matrix products: 8.97 us -> 0 us
  waiting for transfers between devices: 74.7 us -> 66.4 us
  starting transfers between devices: 12.9 us -> 16.5 us
  between operations: 7.25 us -> 4.58 us
    concatenate x2 -> x0, other arithmetic: 27 us -> none  [shards(): jnp.concatenate([from_left[m], buffers[m], from_right[m]], axis=0)]
    pallas_call x0 -> x3, Pallas kernels: none -> 21 us  [the longest x1 11.4 us: finish(): pl.pallas_call(finish_kernel, grid_spec=pltpu.PrefetchScalarGridSpec(num_...]
    another operation x4 -> x0, other arithmetic: 11 us -> none  [the longest x3 10.8 us: shards(): aligned = jnp.stack(aligned_list)]
    gather x2 -> x0, local copies, waits for them, and re-layouts: 10.6 us -> none  [the longest x1 5.28 us: shards(): gathered = incoming[position]]
    dot_general x1 -> x0, matrix products: 8.97 us -> none  [shards(): jnp.dot(stored.reshape(slot_count * BLOCK, n_data * col_width), probe, pr...]
    ppermute x2, waiting for transfers between devices: 23.8 us -> 15.5 us  [from_behind(): return lax.ppermute(block, axis, route)]
    transpose x1 -> x0, local copies, waits for them, and re-layouts: 6.39 us -> none  [shards(): gathered.transpose(0, 2, 1, 3)]
    unnamed x9 -> x4, local copies, waits for them, and re-layouts: 6.42 us -> 0.97 us
  transfers between devices with their start and end apart: 3 -> 3, of which waited for: 3 -> 2; matrix products, arithmetic and copies ran while one was open for 1% -> 1% of each run, Pallas kernels for 0% -> 5%
where the time goes in v1:
time: 116 us; the launch traced here: 115 us
  waiting for transfers between devices  66.4 us (57%)
  Pallas kernels  21 us (18%)
  starting transfers between devices  16.5 us (14%)
  between operations  4.58 us (4%)
  local copies, waits for them, and re-layouts  3.29 us (3%)
  other arithmetic  3.18 us (3%)
    all_to_all x1, waiting for transfers between devices, shards(): lax.all_to_all(outgoing, ('dp', 'tensor'), split_axis=0, concat_axis=0, t...  50.9 us
    ppermute x2, waiting for transfers between devices, from_behind(): return lax.ppermute(block, axis, route)  15.5 us
    pallas_call x1, Pallas kernels, finish(): pl.pallas_call(finish_kernel, grid_spec=pltpu.PrefetchScalarGridSpec(num_...  11.4 us
    all_to_all x1, starting transfers between devices, shards(): lax.all_to_all(outgoing, ('dp', 'tensor'), split_axis=0, concat_axis=0, t...  10.6 us
    pallas_call x1, Pallas kernels, pack_own(): pl.pallas_call(functools.partial(own_kernel, quarter), grid_spec=pltpu.Pr...  6.26 us
    ppermute x2, starting transfers between devices, from_behind(): return lax.ppermute(block, axis, route)  5.9 us
    pallas_call x1, Pallas kernels, patch(): pl.pallas_call(functools.partial(patch_kernel, quarter), grid_spec=pltpu....  3.38 us
  transfers between devices with their start and end apart: 3, of which 2 were waited for; matrix products, arithmetic and copies ran while one was open for 1% of the time, Pallas kernels for 5%

profile of v1, /device:TPU:1, one launch (start us, length us, event | category | flops | bytes accessed | tf_op | source)
XLA Modules:
  0.0 115.0 jit_solution(7019052113922752703)
XLA Ops:
  0.6 1.5 %subtract_reduce_fusion = (s32[2]{0:T(128)}, s32[2]{0:T(128)}, s32[2,1]{1,0:T(2,128)S(1)}) fusion(s32[2,17]{1,0:T(2,128)} %param.7, s32[]{:T(128)S(6)} %select_n.63, s32[]{:T(128)S(6)} %mul.28, s32[]{:T(128)S(6)} %select_n.62, s32[]{:T(128)S(6)} %mul.32), kind=kLoop, calls=%fused_computation.27 | loop fusion | flops 8 | bytes 56 | tf_op jit(solution)/shard_map/sub | solution.py:257
  2.2 0.5 fusion.7
  6.6 0.0 copy-start.1
  6.6 1.8 %slice_bitcast_fusion = (bf16[1,2048,128]{2,1,0:T(8,128)(2,1)S(1)}, bf16[1,2048,128]{2,1,0:T(8,128)(2,1)S(1)}, bf16[1,2048,128]{2,1,0:T(8,128)(2,1)S(1)}, bf16[1,2048,128]{2,1,0:T(8,128)(2,1)S(1)}) fusion(bf16[12288,128]{1,0:T(8,128)(2,1)} %head.1, s32[]{:T(128)S(6)} %select_n.69, bf16[12288,128]{1,0:T(8,128)(2,1)} %embed.1, s32[]{:T(128)S(6)} %select_n.68), kind=kLoop, calls=%fused_computation.3 | loop fusion | bytes 4194312 | tf_op jit(solution)/shard_map/stack | solution.py:258
  8.4 0.1 pad_maximum_fusion
  8.5 2.1 %collective-permute-start = (bf16[2,2048,128]{2,1,0:T(8,128)(2,1)S(1)}, bf16[2,2048,128]{2,1,0:T(8,128)(2,1)S(1)}, u32[]{:S(2)}, u32[]{:S(2)}) collective-permute-start(bf16[2,2048,128]{2,1,0:T(8,128)(2,1)S(1)} %pad_maximum_fusion), channel_id=1, source_target_pairs={{15,0},{0,1},{1,2},{2,3},{3,4},{4,5},{5,6},{6,7},{7,8},{8,9},{9,10... | collective-permute-start | bytes 3145736 | tf_op jit(solution)/shard_map/ppermute | solution.py:18
  10.6 0.1 pad_maximum_fusion.1
  10.7 3.8 %collective-permute-start.1 = (bf16[2,2048,128]{2,1,0:T(8,128)(2,1)S(1)}, bf16[2,2048,128]{2,1,0:T(8,128)(2,1)}, u32[]{:S(2)}, u32[]{:S(2)}) collective-permute-start(bf16[2,2048,128]{2,1,0:T(8,128)(2,1)S(1)} %pad_maximum_fusion.1), channel_id=1, source_target_pairs={{1,0},{2,1},{3,2},{4,3},{5,4},{6,5},{7,6},{8,7},{9,8},{10,9},{11,1... | collective-permute-start | bytes 3145736 | tf_op jit(solution)/shard_map/ppermute | solution.py:18
  14.5 0.0 copy-done.1
  14.5 0.8 select_reduce_fusion.dest
  15.3 6.3 %shard_map.68._ = bf16[128,128,128]{2,1,0:T(8,128)(2,1)} custom-call(s32[2]{0:T(128)} %get-tuple-element.3.before, s32[128]{0:T(128)} %select_reduce_fusion.dest, bf16[12288,128]{1,0:T(8,128)(2,1)} %embed.1, bf16[12288,128]{1,0:T(8,128)(2,1)} %head.1), custom_call_target="tpu_custom_call" | custom-call | bytes 10485760 | tf_op jit(solution)/shard_map/pallas_call | solution.py:68
  21.6 15.5 %collective-permute-done.left = bf16[2,2048,128]{2,1,0:T(8,128)(2,1)S(1)} collective-permute-done((bf16[2,2048,128]{2,1,0:T(8,128)(2,1)S(1)}, bf16[2,2048,128]{2,1,0:T(8,128)(2,1)S(1)}, u32[]{:S(2)}, u32[]{:S(2)}) %collective-permute-start) | collective-permute-done | bytes 1048608 | tf_op jit(solution)/shard_map/ppermute | solution.py:18
  37.1 0.0 copy-start
  37.1 0.0 collective-permute-done.1.right
  37.1 1.0 copy-done
  38.1 3.4 %shard_map.69 = bf16[128,128,128]{2,1,0:T(8,128)(2,1)} custom-call(s32[2]{0:T(128)} %get-tuple-element.3.before, s32[2]{0:T(128)} %get-tuple-element.2.after, s32[128]{0:T(128)} %select_reduce_fusion.dest, bf16[2,2048,128]{2,1,0:T(8,128)(2,1)} %copy-done, bf16[2,2048,128]{2,1,0:T(8,128)(2,1)} %collective-permute-done.1.right, ...), custom_call_target="tpu_custom_call", output_to_operand_aliasing={{}: (5, {})} | custom-call | bytes 6291456 | tf_op jit(solution)/shard_map/pallas_call | solution.py:173
  41.5 10.6 %all-to-all-start = ((bf16[128,128,128]{2,1,0:T(8,128)(2,1)}), bf16[128,128,128]{2,1,0:T(8,128)(2,1)}, u32[]{:S(2)}, u32[]{:S(2)}) async-start(bf16[128,128,128]{2,1,0:T(8,128)(2,1)} %shard_map.69), calls=%async_computation | async-start | bytes 8388608 | tf_op jit(solution)/shard_map/all_to_all | solution.py:278
  52.1 0.6 and_select_fusion.2.source
  52.8 50.9 %all-to-all-done = bf16[128,128,128]{2,1,0:T(8,128)(2,1)} async-done(((bf16[128,128,128]{2,1,0:T(8,128)(2,1)}), bf16[128,128,128]{2,1,0:T(8,128)(2,1)}, u32[]{:S(2)}, u32[]{:S(2)}) %all-to-all-start) | async-done | bytes 4194336 | tf_op jit(solution)/shard_map/all_to_all | solution.py:278
  103.6 11.4 %shard_map.70 = (bf16[16,128,1024]{2,1,0:T(8,128)(2,1)}, f32[16,128,1024]{2,1,0:T(8,128)}) custom-call(s32[16]{0:T(128)} %and_select_fusion.2.source, bf16[8,16,128,128]{3,2,1,0:T(8,128)(2,1)} %bitcast.6.refs_0_.refs_1_, bf16[8,16,128,128]{3,2,1,0:T(8,128)(2,1)} %bitcast.6.refs_0_.refs_1_, bf16[1024,1024]{1,0:T(8,128)(2,1)} %refs_2_.1), custom_call_target="tpu_custom_call" | custom-call | flops 4294967296 | bytes 18874368 | tf_op jit(solution)/shard_map/pallas_call | solution.py:222
  (2 shorter events, 0.0 us)
Async XLA Ops:
  6.6 7.9 %copy-start.1 = (s32[2048]{0:T(1024)S(1)}, s32[2048]{0:T(1024)}, u32[]{:S(2)}) copy-start(s32[2048]{0:T(1024)} %param.8) | copy-start | bytes 24580
  8.5 28.7 %collective-permute-start = (bf16[2,2048,128]{2,1,0:T(8,128)(2,1)S(1)}, bf16[2,2048,128]{2,1,0:T(8,128)(2,1)S(1)}, u32[]{:S(2)}, u32[]{:S(2)}) collective-permute-start(bf16[2,2048,128]{2,1,0:T(8,128)(2,1)S(1)} %pad_maximum_fusion), channel_id=1, source_target_pairs={{15,0},{0,1},{1,2},{2,3},{3,4},{4,5},{5,6},{6,7},{7,8},{8,9},{9,10... | collective-permute-start | bytes 3145736 | tf_op jit(solution)/shard_map/ppermute | solution.py:18
  10.7 26.5 %collective-permute-start.1 = (bf16[2,2048,128]{2,1,0:T(8,128)(2,1)S(1)}, bf16[2,2048,128]{2,1,0:T(8,128)(2,1)}, u32[]{:S(2)}, u32[]{:S(2)}) collective-permute-start(bf16[2,2048,128]{2,1,0:T(8,128)(2,1)S(1)} %pad_maximum_fusion.1), channel_id=1, source_target_pairs={{1,0},{2,1},{3,2},{4,3},{5,4},{6,5},{7,6},{8,7},{9,8},{10,9},{11,1... | collective-permute-start | bytes 3145736 | tf_op jit(solution)/shard_map/ppermute | solution.py:18
  37.1 1.0 copy-start
  41.5 62.1 %all-to-all-start = ((bf16[128,128,128]{2,1,0:T(8,128)(2,1)}), bf16[128,128,128]{2,1,0:T(8,128)(2,1)}, u32[]{:S(2)}, u32[]{:S(2)}) async-start(bf16[128,128,128]{2,1,0:T(8,128)(2,1)} %shard_map.69), calls=%async_computation | async-start | bytes 8388608 | tf_op jit(solution)/shard_map/all_to_all | solution.py:278

commit v2 on v1

--- a/solution.py
+++ b/solution.py
@@ -1,4 +1,6 @@
 import functools
+import itertools
+import random
 
 import jax
 import jax.numpy as jnp
@@ -194,6 +196,62 @@
     )(before, after, dest, left, right, outgoing)
 
 
+MESH = pl.DeviceIdType.MESH
+Z = 4
+Y = 4
+X = 4
+
+
+def exchange_order():
+    offsets = list(itertools.product(range(Z), range(2), range(Y), range(X)))[1:]
+    random.Random(0).shuffle(offsets)
+    return sorted(offsets, key=lambda o: -sum(min(a, 4 - a) for a in (o[0], o[2], o[3])))
+
+
+def exchange_kernel(order, outgoing, incoming, send_sem, recv_sem, own_sem):
+    data = lax.axis_index("dp")
+    tensor = lax.axis_index("tensor")
+    me = data * (Y * X) + tensor
+    z, core, y, x = data // 2, data % 2, tensor // X, tensor % X
+
+    def peer(offset):
+        dz, dc, dy, dx = offset
+        return (((z + dz) % Z) * 2 + (core + dc) % 2, ((y + dy) % Y) * X + (x + dx) % X)
+
+    barrier = pltpu.get_barrier_semaphore()
+    for offset in order:
+        pl.semaphore_signal(barrier, inc=1, device_id=peer(offset), device_id_type=MESH)
+    own = pltpu.make_async_copy(outgoing.at[me], incoming.at[me], own_sem)
+    own.start()
+    count = len(order)
+    pl.semaphore_wait(barrier, count)
+    for offset in order:
+        target = peer(offset)
+        pltpu.make_async_remote_copy(
+            src_ref=outgoing.at[target[0] * (Y * X) + target[1]],
+            dst_ref=incoming.at[me],
+            send_sem=send_sem,
+            recv_sem=recv_sem,
+            device_id=target,
+            device_id_type=MESH,
+        ).start()
+    own.wait()
+    sent, got = outgoing.at[pl.ds(0, count)], incoming.at[pl.ds(0, count)]
+    pltpu.make_async_copy(got, got, recv_sem).wait()
+    pltpu.make_async_copy(sent, sent, send_sem).wait()
+
+
+def exchange(outgoing):
+    return pl.pallas_call(
+        functools.partial(exchange_kernel, exchange_order()),
+        in_specs=[pl.BlockSpec(memory_space=pl.ANY)],
+        out_specs=pl.BlockSpec(memory_space=pl.ANY),
+        out_shape=jax.ShapeDtypeStruct(outgoing.shape, outgoing.dtype),
+        scratch_shapes=[pltpu.SemaphoreType.DMA] * 3,
+        compiler_params=pltpu.CompilerParams(collective_id=0, has_side_effects=True),
+    )(outgoing)
+
+
 PAIR = 2
 
 
@@ -275,7 +333,7 @@
 
     outgoing = pack_own(embed_rows, head_rows, before, dest, quarter)
     outgoing = patch(outgoing, from_left, from_right, before, after, dest)
-    incoming = lax.all_to_all(outgoing, ("dp", "tensor"), split_axis=0, concat_axis=0, tiled=True)
+    incoming = exchange(outgoing)
     writer = my_data * n_tensor + my_tensor
     mine = lax.dynamic_slice_in_dim(slot_table, writer * slot_count, slot_count)
     source = mine % total_blocks // per_rank

time: 116 us -> 113 us (0.974)
  the two profiles are of different devices: /device:TPU:1 before, /device:TPU:26 now
where the time goes in v2:
time: 113 us
  Pallas kernels  84.1 us (74%)
  waiting for transfers between devices  16.5 us (15%)
  between operations  4.57 us (4%)
  other arithmetic  3.14 us (3%)
  local copies, waits for them, and re-layouts  2.33 us (2%)
  starting transfers between devices  2.16 us (2%)
    pallas_call x1, Pallas kernels, exchange(): pl.pallas_call(functools.partial(exchange_kernel, exchange_order()), in_s...  63.3 us
    ppermute x2, waiting for transfers between devices, from_behind(): return lax.ppermute(block, axis, route)  16.5 us
    pallas_call x1, Pallas kernels, finish(): pl.pallas_call(finish_kernel, grid_spec=pltpu.PrefetchScalarGridSpec(num_...  11.4 us
    pallas_call x1, Pallas kernels, pack_own(): pl.pallas_call(functools.partial(own_kernel, quarter), grid_spec=pltpu.Pr...  6.26 us
    pallas_call x1, Pallas kernels, patch(): pl.pallas_call(functools.partial(patch_kernel, quarter), grid_spec=pltpu....  3.1 us
  transfers between devices with their start and end apart: 2, of which 2 were waited for; matrix products, arithmetic and copies ran while one was open for 1% of the time, Pallas kernels for 6%

profile of v2, /device:TPU:26, one launch (start us, length us, event | category | flops | bytes accessed | tf_op | source)
XLA Modules:
  0.0 112.8 jit_solution(14315534921406825030)
XLA Ops:
  0.6 1.5 %subtract_reduce_fusion = (s32[2]{0:T(128)}, s32[2]{0:T(128)}, s32[2,1]{1,0:T(2,128)S(1)}) fusion(s32[2,17]{1,0:T(2,128)} %param.7, s32[]{:T(128)S(6)} %select_n.63, s32[]{:T(128)S(6)} %mul.28, s32[]{:T(128)S(6)} %select_n.62, s32[]{:T(128)S(6)} %mul.32), kind=kLoop, calls=%fused_computation.27 | loop fusion | flops 8 | bytes 56 | tf_op jit(solution)/shard_map/sub | solution.py:315
  2.2 0.5 fusion.7
  6.6 0.0 copy-start.1
  6.6 1.8 %slice_bitcast_fusion = (bf16[1,2048,128]{2,1,0:T(8,128)(2,1)S(1)}, bf16[1,2048,128]{2,1,0:T(8,128)(2,1)S(1)}, bf16[1,2048,128]{2,1,0:T(8,128)(2,1)S(1)}, bf16[1,2048,128]{2,1,0:T(8,128)(2,1)S(1)}) fusion(bf16[12288,128]{1,0:T(8,128)(2,1)} %head.1, s32[]{:T(128)S(6)} %select_n.69, bf16[12288,128]{1,0:T(8,128)(2,1)} %embed.1, s32[]{:T(128)S(6)} %select_n.68), kind=kLoop, calls=%fused_computation.3 | loop fusion | bytes 4194312 | tf_op jit(solution)/shard_map/stack | solution.py:316
  8.4 0.1 pad_maximum_fusion
  8.5 1.6 %collective-permute-start = (bf16[2,2048,128]{2,1,0:T(8,128)(2,1)S(1)}, bf16[2,2048,128]{2,1,0:T(8,128)(2,1)S(1)}, u32[]{:S(2)}, u32[]{:S(2)}) collective-permute-start(bf16[2,2048,128]{2,1,0:T(8,128)(2,1)S(1)} %pad_maximum_fusion), channel_id=1, source_target_pairs={{15,0},{0,1},{1,2},{2,3},{3,4},{4,5},{5,6},{6,7},{7,8},{8,9},{9,10... | collective-permute-start | bytes 3145736 | tf_op jit(solution)/shard_map/ppermute | solution.py:20
  10.1 0.1 pad_maximum_fusion.1
  10.2 0.6 collective-permute-start.1
  10.8 0.0 copy-done.1
  10.8 0.8 select_reduce_fusion.dest
  11.6 6.3 %shard_map.68._ = bf16[128,128,128]{2,1,0:T(8,128)(2,1)} custom-call(s32[2]{0:T(128)} %get-tuple-element.3.before, s32[128]{0:T(128)} %select_reduce_fusion.dest, bf16[12288,128]{1,0:T(8,128)(2,1)} %embed.1, bf16[12288,128]{1,0:T(8,128)(2,1)} %head.1), custom_call_target="tpu_custom_call" | custom-call | bytes 10485760 | tf_op jit(solution)/shard_map/pallas_call | solution.py:70
  17.8 0.6 and_select_fusion.2.source
  18.4 15.0 %collective-permute-done.left = bf16[2,2048,128]{2,1,0:T(8,128)(2,1)S(1)} collective-permute-done((bf16[2,2048,128]{2,1,0:T(8,128)(2,1)S(1)}, bf16[2,2048,128]{2,1,0:T(8,128)(2,1)S(1)}, u32[]{:S(2)}, u32[]{:S(2)}) %collective-permute-start) | collective-permute-done | bytes 1048608 | tf_op jit(solution)/shard_map/ppermute | solution.py:20
  33.5 0.0 copy-start
  33.5 1.5 %collective-permute-done.1.right = bf16[2,2048,128]{2,1,0:T(8,128)(2,1)} collective-permute-done((bf16[2,2048,128]{2,1,0:T(8,128)(2,1)S(1)}, bf16[2,2048,128]{2,1,0:T(8,128)(2,1)}, u32[]{:S(2)}, u32[]{:S(2)}) %collective-permute-start.1) | collective-permute-done | bytes 1048608 | tf_op jit(solution)/shard_map/ppermute | solution.py:20
  34.9 0.0 copy-done
  34.9 3.1 %shard_map.69.outgoing = bf16[128,128,128]{2,1,0:T(8,128)(2,1)} custom-call(s32[2]{0:T(128)} %get-tuple-element.3.before, s32[2]{0:T(128)} %get-tuple-element.2.after, s32[128]{0:T(128)} %select_reduce_fusion.dest, bf16[2,2048,128]{2,1,0:T(8,128)(2,1)} %copy-done, ...), custom_call_target="tpu_custom_call", output_to_operand_aliasing={{}: (5, {})} | custom-call | bytes 6291456 | tf_op jit(solution)/shard_map/pallas_call | solution.py:175
  38.1 63.3 %shard_map.70 = bf16[128,128,128]{2,1,0:T(8,128)(2,1)} custom-call(bf16[128,128,128]{2,1,0:T(8,128)(2,1)} %shard_map.69.outgoing), custom_call_target="tpu_custom_call" | custom-call | tf_op jit(solution)/shard_map/pallas_call | solution.py:245
  101.4 11.4 %shard_map.71 = (bf16[16,128,1024]{2,1,0:T(8,128)(2,1)}, f32[16,128,1024]{2,1,0:T(8,128)}) custom-call(s32[16]{0:T(128)} %and_select_fusion.2.source, bf16[8,16,128,128]{3,2,1,0:T(8,128)(2,1)} %bitcast.11, bf16[8,16,128,128]{3,2,1,0:T(8,128)(2,1)} %bitcast.12, bf16[1024,1024]{1,0:T(8,128)(2,1)} %refs_2_.1), custom_call_target="tpu_custom_call" | custom-call | flops 4294967296 | bytes 18874368 | tf_op jit(solution)/shard_map/pallas_call | solution.py:280
  (2 shorter events, 0.0 us)
Async XLA Ops:
  6.6 4.2 %copy-start.1 = (s32[2048]{0:T(1024)S(1)}, s32[2048]{0:T(1024)}, u32[]{:S(2)}) copy-start(s32[2048]{0:T(1024)} %param.8) | copy-start | bytes 24580
  8.5 25.0 %collective-permute-start = (bf16[2,2048,128]{2,1,0:T(8,128)(2,1)S(1)}, bf16[2,2048,128]{2,1,0:T(8,128)(2,1)S(1)}, u32[]{:S(2)}, u32[]{:S(2)}) collective-permute-start(bf16[2,2048,128]{2,1,0:T(8,128)(2,1)S(1)} %pad_maximum_fusion), channel_id=1, source_target_pairs={{15,0},{0,1},{1,2},{2,3},{3,4},{4,5},{5,6},{6,7},{7,8},{8,9},{9,10... | collective-permute-start | bytes 3145736 | tf_op jit(solution)/shard_map/ppermute | solution.py:20
  10.2 24.8 %collective-permute-start.1 = (bf16[2,2048,128]{2,1,0:T(8,128)(2,1)S(1)}, bf16[2,2048,128]{2,1,0:T(8,128)(2,1)}, u32[]{:S(2)}, u32[]{:S(2)}) collective-permute-start(bf16[2,2048,128]{2,1,0:T(8,128)(2,1)S(1)} %pad_maximum_fusion.1), channel_id=1, source_target_pairs={{1,0},{2,1},{3,2},{4,3},{5,4},{6,5},{7,6},{8,7},{9,8},{10,9},{11,1... | collective-permute-start | bytes 3145736 | tf_op jit(solution)/shard_map/ppermute | solution.py:20
  33.5 1.5 %copy-start = (bf16[2,2048,128]{2,1,0:T(8,128)(2,1)}, bf16[2,2048,128]{2,1,0:T(8,128)(2,1)S(1)}, u32[]{:S(2)}) copy-start(bf16[2,2048,128]{2,1,0:T(8,128)(2,1)S(1)} %collective-permute-done.left) | copy-start | bytes 3145732

commit v3 on v0

v3 whole, which is shorter than its diff:
```python
import functools
import itertools
import random

import jax
import jax.numpy as jnp
from jax import lax
from jax.experimental import pallas as pl
from jax.experimental.pallas import tpu as pltpu
from jax.sharding import PartitionSpec as P

R = 8192
BLOCK = 128
MESH = pl.DeviceIdType.MESH
Z = 4
Y = 4
X = 4
QUARTER = R // 4
LIFT = 16
TRAIL = QUARTER + LIFT
HIGH = R - QUARTER
PAD = BLOCK
OWN = PAD + R + QUARTER
FOREIGN = PAD + TRAIL
PACK = 8


def exchange_order():
    offsets = list(itertools.product(range(Z), range(2), range(Y), range(X)))[1:]
    random.Random(0).shuffle(offsets)
    offsets.sort(key=lambda o: -sum(min(a, 4 - a) for a in (o[0], o[2], o[3])))
    return offsets + [(0, 0, 0, 0)]


ORDER = exchange_order()


def save_kernel(
    offsets, picked, embed, head, incoming, low, high, own, arrived, foreign, trail, packed,
    load_sem, shift_send, shift_recv, send_sem, recv_sem, own_sem, plane_sem, space_sem,
):
    data = lax.axis_index("dp")
    tensor = lax.axis_index("tensor")
    me = data * (Y * X) + tensor
    z, core, y, x = data // 2, data % 2, tensor // X, tensor % X
    ranks = Y * X
    following = (data, (tensor + 1) % ranks)
    previous = (data, (tensor + ranks - 1) % ranks)

    def peer(offset):
        dz, dc, dy, dx = offset
        return (((z + dz) % Z) * 2 + (core + dc) % 2, ((y + dy) % Y) * X + (x + dx) % X)

    def signal(sem, device):
        pl.semaphore_signal(sem, inc=1, device_id=device, device_id_type=MESH)

    sources = (embed, head)
    height = embed.shape[0]

    def load(m, part):
        if part == 0:
            return pltpu.make_async_copy(
                sources[m].at[pl.ds(HIGH, height - HIGH)],
                high.at[pl.ds(m * (height - HIGH), height - HIGH)],
                load_sem.at[0, m],
            )
        return pltpu.make_async_copy(sources[m].at[pl.ds(0, HIGH)], low.at[m], load_sem.at[1, m])

    row = [(0, dc, 0, dx) for dc in range(2) for dx in range(X) if (dc, dx) != (0, 0)]
    column = [(0, 0, d, 0) for d in range(1, Y)]
    stack = [(d, 0, 0, 0) for d in range(1, Z)]
    barrier = pltpu.get_barrier_semaphore()
    signal(barrier, following)
    signal(barrier, previous)
    for offset in stack + column + row:
        signal(barrier, peer(offset))
    for part in range(2):
        for m in range(2):
            load(m, part).start()
    pl.semaphore_wait(barrier, 2 + len(stack + column + row))

    def lead(m):
        return pltpu.make_async_remote_copy(
            src_ref=sources[m].at[pl.ds(0, QUARTER)],
            dst_ref=arrived.at[m, 1, pl.ds(0, QUARTER)],
            send_sem=shift_send.at[1, m],
            recv_sem=shift_recv.at[1, m],
            device_id=previous,
            device_id_type=MESH,
        )

    def tail(m):
        return pltpu.make_async_remote_copy(
            src_ref=trail.at[m],
            dst_ref=arrived.at[m, 0],
            send_sem=shift_send.at[0, m],
            recv_sem=shift_recv.at[0, m],
            device_id=following,
            device_id_type=MESH,
        )

    lead(0).start()
    lead(1).start()
    load(0, 0).wait()
    load(1, 0).wait()
    for m in range(2):
        begin = (tensor + 1) * R - offsets[m, tensor] - HIGH
        begin = jnp.clip(begin, 0, height - HIGH - TRAIL + LIFT - 1)
        begin = lax.div(begin, LIFT) * LIFT
        begin = m * (height - HIGH) + begin
        trail[m] = high[pl.ds(begin, TRAIL), :]
    tail(0).start()
    tail(1).start()

    for offset in column:
        signal(plane_sem, peer(offset))
    pl.semaphore_wait(plane_sem, len(column))
    for offset in stack:
        signal(space_sem, peer(offset))
    load(0, 1).wait()
    load(1, 1).wait()
    step = 256
    for m in range(2):

        @pl.loop(0, HIGH // step)
        def _(i):
            at = pl.multiple_of(i * step, step)
            own[pl.ds(m * OWN + PAD + at, step), :] = low[m, pl.ds(at, step), :].astype(jnp.float32)

        @pl.loop(0, (R + QUARTER - HIGH) // step)
        def _(i):
            at = pl.multiple_of(i * step, step)
            rows = high[pl.ds(m * (height - HIGH) + at, step), :]
            own[pl.ds(m * OWN + PAD + HIGH + at, step), :] = rows.astype(jnp.float32)

    pl.semaphore_wait(space_sem, len(stack))

    for m in range(2):
        for side in range(2):
            (tail, lead)[side](m).wait_recv()

            @pl.loop(0, TRAIL // (3 * LIFT))
            def _(i):
                at = pl.multiple_of(i * 3 * LIFT, LIFT)
                rows = arrived[m, side, pl.ds(at, 3 * LIFT), :].astype(jnp.float32)
                foreign[pl.ds((m * 2 + side) * FOREIGN + PAD + at, 3 * LIFT), :] = rows

    earlier = (tensor + ranks - 1) % ranks
    befores = [offsets[m, tensor] - tensor * R for m in range(2)]
    afters = [offsets[m, tensor + 1] - tensor * R for m in range(2)]
    lifts = [lax.rem((earlier + 1) * R - offsets[m, earlier], LIFT) for m in range(2)]
    local_row = lax.broadcasted_iota(jnp.int32, (BLOCK, embed.shape[1]), 0)

    def pack(k):
        local = picked[k]
        m = lax.div(local, R // BLOCK)
        block = lax.rem(local, R // BLOCK)
        first = block * BLOCK
        before = befores[0] + m * (befores[1] - befores[0])
        after = afters[0] + m * (afters[1] - afters[0])
        lift = lifts[0] + m * (lifts[1] - lifts[0])
        own_at = m * OWN + PAD + jnp.clip(first - before, -PAD, R + QUARTER - BLOCK)
        left_at = jnp.clip(first + lift, -PAD, TRAIL - BLOCK)
        right_at = jnp.clip(first - after, -PAD, TRAIL - BLOCK)
        side = lax.div(block, R // BLOCK // 2)
        at = (m * 2 + side) * FOREIGN + PAD + left_at + side * (right_at - left_at)
        mine = own[pl.ds(own_at, BLOCK), :]
        theirs = foreign[pl.ds(at, BLOCK), :]
        keep = (local_row >= before - first) & (local_row < after - first)
        packed[k] = jnp.where(keep, mine, theirs).astype(packed.dtype)

    def send(k):
        return pltpu.make_async_remote_copy(
            src_ref=packed.at[k],
            dst_ref=incoming.at[me],
            send_sem=send_sem,
            recv_sem=recv_sem,
            device_id=peer(ORDER[k]),
            device_id_type=MESH,
        )

    count = len(ORDER)
    for group in range(0, count + PACK, PACK):
        if group < count:

            @pl.loop(group, group + PACK)
            def _(k):
                pack(k)

        for k in range(max(group - PACK, 0), min(group, count - 1)):
            send(k).start()
    own_copy = pltpu.make_async_copy(packed.at[count - 1], incoming.at[me], own_sem)
    own_copy.start()
    own_copy.wait()
    got, sent = incoming.at[pl.ds(0, count - 1)], packed.at[pl.ds(0, count - 1)]
    pltpu.make_async_copy(got, got, recv_sem).wait()
    pltpu.make_async_copy(sent, sent, send_sem).wait()
    for m in range(2):
        lead(m).wait_send()
        tail(m).wait_send()


def save(embed_rows, head_rows, row_offsets, picked):
    height, width = embed_rows.shape
    dtype = embed_rows.dtype
    return pl.pallas_call(
        save_kernel,
        grid_spec=pltpu.PrefetchScalarGridSpec(
            num_scalar_prefetch=2,
            grid=(),
            in_specs=[pl.BlockSpec(memory_space=pl.ANY)] * 2,
            out_specs=pl.BlockSpec(memory_space=pl.ANY),
            scratch_shapes=[
                pltpu.VMEM((2, HIGH, width), dtype),
                pltpu.VMEM((2 * (height - HIGH), width), dtype),
                pltpu.VMEM((2 * OWN, width), jnp.float32),
                pltpu.VMEM((2, 2, TRAIL, width), dtype),
                pltpu.VMEM((4 * FOREIGN, width), jnp.float32),
                pltpu.VMEM((2, TRAIL, width), dtype),
                pltpu.VMEM((len(ORDER), BLOCK, width), dtype),
                pltpu.SemaphoreType.DMA((2, 2)),
                pltpu.SemaphoreType.DMA((2, 2)),
                pltpu.SemaphoreType.DMA((2, 2)),
                pltpu.SemaphoreType.DMA,
                pltpu.SemaphoreType.DMA,
                pltpu.SemaphoreType.DMA,
                pltpu.SemaphoreType.REGULAR,
                pltpu.SemaphoreType.REGULAR,
            ],
        ),
        out_shape=jax.ShapeDtypeStruct((len(ORDER), BLOCK, width), dtype),
        compiler_params=pltpu.CompilerParams(collective_id=0, has_side_effects=True),
    )(row_offsets, picked, embed_rows, head_rows)


PAIR = 2


def finish_kernel(source, *refs):
    pieces = refs[:PAIR]
    probe, stored, sketch = refs[PAIR:]
    n_data, height, width = pieces[0].shape
    for i in range(PAIR):
        for d in range(n_data):
            stored[i, :, d * width:(d + 1) * width] = pieces[i][d]
    x = stored[...].reshape(PAIR * height, n_data * width)
    y = jnp.dot(x, probe[...], preferred_element_type=jnp.float32)
    sketch[...] = y.reshape(sketch.shape)


def finish(incoming, probe, source):
    n_data, n_tensor, height, width = incoming.shape
    slots = source.shape[0]
    columns = n_data * width

    def piece(i):
        return pl.BlockSpec(
            (n_data, None, height, width), lambda g, source: (0, source[g * PAIR + i], 0, 0)
        )

    return pl.pallas_call(
        finish_kernel,
        grid_spec=pltpu.PrefetchScalarGridSpec(
            num_scalar_prefetch=1,
            grid=(slots // PAIR,),
            in_specs=[piece(i) for i in range(PAIR)]
            + [pl.BlockSpec(probe.shape, lambda g, source: (0, 0))],
            out_specs=[
                pl.BlockSpec((PAIR, height, columns), lambda g, source: (g, 0, 0)),
                pl.BlockSpec((PAIR, height, probe.shape[1]), lambda g, source: (g, 0, 0)),
            ],
        ),
        out_shape=[
            jax.ShapeDtypeStruct((slots, height, columns), incoming.dtype),
            jax.ShapeDtypeStruct((slots, height, probe.shape[1]), jnp.float32),
        ],
        cost_estimate=pl.CostEstimate(
            flops=2 * slots * height * columns * probe.shape[1],
            bytes_accessed=18 << 20,
            transcendentals=0,
        ),
    )(source, *([incoming] * PAIR), probe)


def shards(embed_rows, head_rows, row_offsets, slot_table, probe):
    n_tensor = lax.axis_size("tensor")
    n_data = lax.axis_size("dp")
    tensor = lax.axis_index("tensor")
    data = lax.axis_index("dp")
    width = embed_rows.shape[1]
    per_rank = R // BLOCK
    total_blocks = per_rank * n_tensor
    slot_count = 2 * total_blocks // (n_tensor * n_data)

    dz, dc, dy, dx = (jnp.array(steps, jnp.int32) for steps in zip(*ORDER))
    target = ((data // 2 + dz) % Z * 2 + (data + dc) % 2) * n_tensor
    target = target + (tensor // X + dy) % Y * X + (tensor + dx) % X
    holder = jnp.arange(2 * total_blocks, dtype=jnp.int32) // slot_count
    local = jnp.where(
        slot_table % total_blocks // per_rank == tensor,
        slot_table // total_blocks * per_rank + slot_table % per_rank,
        0,
    )
    picked = jnp.sum(jnp.where(holder[None, :] == target[:, None], local[None, :], 0), axis=1)

    incoming = save(embed_rows, head_rows, row_offsets, picked.astype(jnp.int32))
    incoming = incoming.reshape(n_data, n_tensor, BLOCK, width)
    writer = data * n_tensor + tensor
    mine = lax.dynamic_slice_in_dim(slot_table, writer * slot_count, slot_count)
    source = mine % total_blocks // per_rank
    stored, sketch = finish(incoming, probe, source)
    return (stored, sketch)


def solution(mesh):
    return jax.shard_map(
        shards,
        mesh=mesh,
        in_specs=(P("tensor", "dp"), P("tensor", "dp"), P(), P(), P()),
        out_specs=(P(("dp", "tensor"), None, None), P(("dp", "tensor"), None, None)),
        check_vma=False,
    )
```

time: 174 us -> 102 us (0.59)
  Pallas kernels: 0 us -> 97.1 us
  waiting for transfers between devices: 74.7 us -> 0 us
  other arithmetic: 41.5 us -> 3.5 us
  local copies, waits for them, and re-layouts: 27.9 us -> 0 us
  starting transfers between devices: 12.9 us -> 0 us
  matrix products: 8.97 us -> 0 us
  between operations: 7.25 us -> 0.67 us
    pallas_call x0 -> x2, Pallas kernels: none -> 97.1 us  [the longest x1 85.7 us: save(): pl.pallas_call(save_kernel, grid_spec=pltpu.PrefetchScalarGridSpec(num_sc...]
    all_to_all x1 -> x0, waiting for transfers between devices: 50.9 us -> none  [shards(): lax.all_to_all(outgoing, ('dp', 'tensor'), split_axis=0, concat_axis=0, t...]
    concatenate x2 -> x0, other arithmetic: 27 us -> none  [shards(): jnp.concatenate([from_left[m], buffers[m], from_right[m]], axis=0)]
    ppermute x2 -> x0, waiting for transfers between devices: 23.8 us -> none  [from_behind(): return lax.ppermute(block, axis, route)]
    another operation x6 -> x0, other arithmetic: 13.2 us -> none  [the longest x3 10.8 us: shards(): aligned = jnp.stack(aligned_list)]
    gather x2 -> x0, local copies, waits for them, and re-layouts: 10.6 us -> none  [the longest x1 5.28 us: shards(): gathered = incoming[position]]
    dot_general x1 -> x0, matrix products: 8.97 us -> none  [shards(): jnp.dot(stored.reshape(slot_count * BLOCK, n_data * col_width), probe, pr...]
    all_to_all x1 -> x0, starting transfers between devices: 7.18 us -> none  [shards(): lax.all_to_all(outgoing, ('dp', 'tensor'), split_axis=0, concat_axis=0, t...]
  transfers between devices with their start and end apart: 3 -> 0, of which waited for: 3 -> 0; matrix products, arithmetic and copies ran while one was open for 1% -> 0% of each run, Pallas kernels for 0% -> 0%
where the time goes in v3:
time: 102 us; the launch traced here: 101 us
  Pallas kernels  97.1 us (95%)
  other arithmetic  3.5 us (3%)
    pallas_call x1, Pallas kernels, save(): pl.pallas_call(save_kernel, grid_spec=pltpu.PrefetchScalarGridSpec(num_sc...  85.7 us
    pallas_call x1, Pallas kernels, finish(): pl.pallas_call(finish_kernel, grid_spec=pltpu.PrefetchScalarGridSpec(num_...  11.4 us

profile of v3, /device:TPU:1, one launch (start us, length us, event | category | flops | bytes accessed | tf_op | source)
XLA Modules:
  0.0 101.3 jit_solution(2700758838732403816)
XLA Ops:
  0.7 1.3 %and_select_fusion.4.source = s32[16]{0:T(128)} fusion(s32[2048]{0:T(1024)} %param.12, s32[]{:T(128)S(6)} %select_n.73), kind=kLoop, calls=%fused_computation.44 | loop fusion | flops 416 | bytes 132 | tf_op jit(solution)/shard_map/jit(floor_divide)/jit(_where)/select_n | solution.py:310
  2.0 0.7 fusion.13
  2.7 0.7 add_select_fusion.4
  3.4 0.8 select_reduce_fusion.picked
  4.2 85.7 %shard_map.104 = bf16[128,128,128]{2,1,0:T(8,128)(2,1)} custom-call(s32[2,17]{1,0:T(2,128)} %offsets.1, s32[128]{0:T(128)} %select_reduce_fusion.picked, bf16[12288,128]{1,0:T(8,128)(2,1)} %embed.1, bf16[12288,128]{1,0:T(8,128)(2,1)} %head.1), custom_call_target="tpu_custom_call" | custom-call | tf_op jit(solution)/shard_map/pallas_call | solution.py:206
  89.9 11.4 %shard_map.105 = (bf16[16,128,1024]{2,1,0:T(8,128)(2,1)}, f32[16,128,1024]{2,1,0:T(8,128)}) custom-call(s32[16]{0:T(128)} %and_select_fusion.4.source, bf16[8,16,128,128]{3,2,1,0:T(8,128)(2,1)} %bitcast.1, bf16[8,16,128,128]{3,2,1,0:T(8,128)(2,1)} %bitcast.2, bf16[1024,1024]{1,0:T(8,128)(2,1)} %refs_2_.1), custom_call_target="tpu_custom_call" | custom-call | flops 4294967296 | bytes 18874368 | tf_op jit(solution)/shard_map/pallas_call | solution.py:261

commit v4 on v3

--- a/solution.py
+++ b/solution.py
@@ -36,8 +36,8 @@
 
 
 def save_kernel(
-    offsets, picked, embed, head, incoming, low, high, own, arrived, foreign, trail, packed,
-    load_sem, shift_send, shift_recv, send_sem, recv_sem, own_sem, plane_sem, space_sem,
+    offsets, table, embed, head, incoming, lookup, picked, low, high, own, arrived, foreign, trail, packed,
+    load_sem, shift_send, shift_recv, send_sem, recv_sem, plane_sem, space_sem,
 ):
     data = lax.axis_index("dp")
     tensor = lax.axis_index("tensor")
@@ -117,6 +117,25 @@
     pl.semaphore_wait(plane_sem, len(column))
     for offset in stack:
         signal(space_sem, peer(offset))
+    per_rank = R // BLOCK
+    slots = table.shape[0] // len(ORDER)
+
+    @pl.loop(0, len(ORDER))
+    def _(j):
+        total = jnp.int32(0)
+        for s in range(slots):
+            number = table[j * slots + s]
+            half = lax.div(number, per_rank * ranks)
+            block = lax.rem(number, per_rank)
+            rank = lax.rem(lax.div(number, per_rank), ranks)
+            other = jnp.minimum(jnp.abs(rank - tensor), 1)
+            total += (half * per_rank + block) * (1 - other)
+        picked[j] = jnp.clip(total, 0, 2 * per_rank - 1)
+
+    for k, offset in enumerate(ORDER):
+        to = peer(offset)
+        lookup[k] = to[0] * ranks + to[1]
+
     load(0, 1).wait()
     load(1, 1).wait()
     step = 256
@@ -152,9 +171,9 @@
     local_row = lax.broadcasted_iota(jnp.int32, (BLOCK, embed.shape[1]), 0)
 
     def pack(k):
-        local = picked[k]
-        m = lax.div(local, R // BLOCK)
-        block = lax.rem(local, R // BLOCK)
+        local = picked[lookup[k]]
+        m = lax.div(local, per_rank)
+        block = lax.rem(local, per_rank)
         first = block * BLOCK
         before = befores[0] + m * (befores[1] - befores[0])
         after = afters[0] + m * (afters[1] - afters[0])
@@ -162,7 +181,7 @@
         own_at = m * OWN + PAD + jnp.clip(first - before, -PAD, R + QUARTER - BLOCK)
         left_at = jnp.clip(first + lift, -PAD, TRAIL - BLOCK)
         right_at = jnp.clip(first - after, -PAD, TRAIL - BLOCK)
-        side = lax.div(block, R // BLOCK // 2)
+        side = lax.div(block, per_rank // 2)
         at = (m * 2 + side) * FOREIGN + PAD + left_at + side * (right_at - left_at)
         mine = own[pl.ds(own_at, BLOCK), :]
         theirs = foreign[pl.ds(at, BLOCK), :]
@@ -189,18 +208,16 @@
 
         for k in range(max(group - PACK, 0), min(group, count - 1)):
             send(k).start()
-    own_copy = pltpu.make_async_copy(packed.at[count - 1], incoming.at[me], own_sem)
-    own_copy.start()
-    own_copy.wait()
-    got, sent = incoming.at[pl.ds(0, count - 1)], packed.at[pl.ds(0, count - 1)]
-    pltpu.make_async_copy(got, got, recv_sem).wait()
-    pltpu.make_async_copy(sent, sent, send_sem).wait()
+    incoming[me] = packed[count - 1]
+    everything = packed.at[pl.ds(0, count - 1)]
+    pltpu.make_async_copy(everything, everything, recv_sem).wait()
+    pltpu.make_async_copy(everything, everything, send_sem).wait()
     for m in range(2):
         lead(m).wait_send()
         tail(m).wait_send()
 
 
-def save(embed_rows, head_rows, row_offsets, picked):
+def save(embed_rows, head_rows, row_offsets, slot_table):
     height, width = embed_rows.shape
     dtype = embed_rows.dtype
     return pl.pallas_call(
@@ -209,8 +226,10 @@
             num_scalar_prefetch=2,
             grid=(),
             in_specs=[pl.BlockSpec(memory_space=pl.ANY)] * 2,
-            out_specs=pl.BlockSpec(memory_space=pl.ANY),
+            out_specs=pl.BlockSpec(memory_space=pltpu.VMEM),
             scratch_shapes=[
+                pltpu.SMEM((len(ORDER),), jnp.int32),
+                pltpu.SMEM((len(ORDER),), jnp.int32),
                 pltpu.VMEM((2, HIGH, width), dtype),
                 pltpu.VMEM((2 * (height - HIGH), width), dtype),
                 pltpu.VMEM((2 * OWN, width), jnp.float32),
@@ -223,92 +242,95 @@
                 pltpu.SemaphoreType.DMA((2, 2)),
                 pltpu.SemaphoreType.DMA,
                 pltpu.SemaphoreType.DMA,
-                pltpu.SemaphoreType.DMA,
                 pltpu.SemaphoreType.REGULAR,
                 pltpu.SemaphoreType.REGULAR,
             ],
         ),
-        out_shape=jax.ShapeDtypeStruct((len(ORDER), BLOCK, width), dtype),
-        compiler_params=pltpu.CompilerParams(collective_id=0, has_side_effects=True),
-    )(row_offsets, picked, embed_rows, head_rows)
-
-
-PAIR = 2
-
-
-def finish_kernel(source, *refs):
-    pieces = refs[:PAIR]
-    probe, stored, sketch = refs[PAIR:]
-    n_data, height, width = pieces[0].shape
-    for i in range(PAIR):
-        for d in range(n_data):
-            stored[i, :, d * width:(d + 1) * width] = pieces[i][d]
-    x = stored[...].reshape(PAIR * height, n_data * width)
-    y = jnp.dot(x, probe[...], preferred_element_type=jnp.float32)
-    sketch[...] = y.reshape(sketch.shape)
-
-
-def finish(incoming, probe, source):
+        out_shape=pltpu.VMEM((len(ORDER), BLOCK, width), dtype),
+        compiler_params=pltpu.CompilerParams(
+            collective_id=0, has_side_effects=True, vmem_limit_bytes=34 << 20
+        ),
+    )(row_offsets, slot_table, embed_rows, head_rows)
+
+
+TAKE = 2
+BUFFERS = 4
+
+
+def finish_kernel(table, incoming, weights, stored, sketch, gathered, product, stored_sem, sketch_sem):
     n_data, n_tensor, height, width = incoming.shape
-    slots = source.shape[0]
+    slots = stored.shape[0]
+    per_rank = R // BLOCK
+    writer = lax.axis_index("dp") * n_tensor + lax.axis_index("tensor")
+    rows = TAKE * height
+
+    def put_stored(g):
+        return pltpu.make_async_copy(
+            gathered.at[pl.ds(g * TAKE, TAKE)], stored.at[pl.ds(g * TAKE, TAKE)], stored_sem.at[g]
+        )
+
+    def put_sketch(g):
+        return pltpu.make_async_copy(
+            product.at[g % BUFFERS], sketch.at[pl.ds(g * rows, rows)], sketch_sem.at[g]
+        )
+
+    groups = slots // TAKE
+    for g in range(groups):
+        for i in range(TAKE):
+            slot = g * TAKE + i
+            rank = lax.rem(lax.div(table[writer * slots + slot], per_rank), n_tensor)
+            for d in range(n_data):
+                gathered[slot, :, d * width:(d + 1) * width] = incoming[d, rank]
+        put_stored(g).start()
+        if g >= BUFFERS:
+            put_sketch(g - BUFFERS).wait()
+        x = gathered[g * TAKE:(g + 1) * TAKE].reshape(rows, n_data * width)
+        product[g % BUFFERS] = jnp.dot(x, weights[...], preferred_element_type=jnp.float32)
+        put_sketch(g).start()
+    for g in range(groups):
+        put_stored(g).wait()
+    for g in range(groups - BUFFERS, groups):
+        put_sketch(g).wait()
+
+
+def finish(incoming, probe, slot_table):
+    n_data, n_tensor, height, width = incoming.shape
+    slots = slot_table.shape[0] // (n_data * n_tensor)
     columns = n_data * width
-
-    def piece(i):
-        return pl.BlockSpec(
-            (n_data, None, height, width), lambda g, source: (0, source[g * PAIR + i], 0, 0)
-        )
-
-    return pl.pallas_call(
+    stored, sketch = pl.pallas_call(
         finish_kernel,
         grid_spec=pltpu.PrefetchScalarGridSpec(
             num_scalar_prefetch=1,
-            grid=(slots // PAIR,),
-            in_specs=[piece(i) for i in range(PAIR)]
-            + [pl.BlockSpec(probe.shape, lambda g, source: (0, 0))],
-            out_specs=[
-                pl.BlockSpec((PAIR, height, columns), lambda g, source: (g, 0, 0)),
-                pl.BlockSpec((PAIR, height, probe.shape[1]), lambda g, source: (g, 0, 0)),
+            grid=(),
+            in_specs=[pl.BlockSpec(memory_space=pltpu.VMEM)] * 2,
+            out_specs=[pl.BlockSpec(memory_space=pl.ANY)] * 2,
+            scratch_shapes=[
+                pltpu.VMEM((slots, height, columns), incoming.dtype),
+                pltpu.VMEM((BUFFERS, TAKE * height, probe.shape[1]), jnp.float32),
+                pltpu.SemaphoreType.DMA((slots // TAKE,)),
+                pltpu.SemaphoreType.DMA((slots // TAKE,)),
             ],
         ),
         out_shape=[
             jax.ShapeDtypeStruct((slots, height, columns), incoming.dtype),
-            jax.ShapeDtypeStruct((slots, height, probe.shape[1]), jnp.float32),
+            jax.ShapeDtypeStruct((slots * height, probe.shape[1]), jnp.float32),
         ],
-        cost_estimate=pl.CostEstimate(
-            flops=2 * slots * height * columns * probe.shape[1],
-            bytes_accessed=18 << 20,
-            transcendentals=0,
-        ),
-    )(source, *([incoming] * PAIR), probe)
+        compiler_params=pltpu.CompilerParams(vmem_limit_bytes=20 << 20),
+    )(slot_table, incoming, probe)
+    return stored, sketch.reshape(slots, height, probe.shape[1])
 
 
 def shards(embed_rows, head_rows, row_offsets, slot_table, probe):
     n_tensor = lax.axis_size("tensor")
     n_data = lax.axis_size("dp")
-    tensor = lax.axis_index("tensor")
-    data = lax.axis_index("dp")
-    width = embed_rows.shape[1]
-    per_rank = R // BLOCK
-    total_blocks = per_rank * n_tensor
-    slot_count = 2 * total_blocks // (n_tensor * n_data)
-
-    dz, dc, dy, dx = (jnp.array(steps, jnp.int32) for steps in zip(*ORDER))
-    target = ((data // 2 + dz) % Z * 2 + (data + dc) % 2) * n_tensor
-    target = target + (tensor // X + dy) % Y * X + (tensor + dx) % X
-    holder = jnp.arange(2 * total_blocks, dtype=jnp.int32) // slot_count
-    local = jnp.where(
-        slot_table % total_blocks // per_rank == tensor,
-        slot_table // total_blocks * per_rank + slot_table % per_rank,
-        0,
+    probe = pltpu.with_memory_space_constraint(probe, pltpu.VMEM)
+    embed_rows, head_rows, row_offsets, slot_table = (
+        pltpu.with_memory_space_constraint(a, pltpu.HBM)
+        for a in (embed_rows, head_rows, row_offsets, slot_table)
     )
-    picked = jnp.sum(jnp.where(holder[None, :] == target[:, None], local[None, :], 0), axis=1)
-
-    incoming = save(embed_rows, head_rows, row_offsets, picked.astype(jnp.int32))
-    incoming = incoming.reshape(n_data, n_tensor, BLOCK, width)
-    writer = data * n_tensor + tensor
-    mine = lax.dynamic_slice_in_dim(slot_table, writer * slot_count, slot_count)
-    source = mine % total_blocks // per_rank
-    stored, sketch = finish(incoming, probe, source)
+    incoming = save(embed_rows, head_rows, row_offsets, slot_table)
+    incoming = incoming.reshape(n_data, n_tensor, BLOCK, embed_rows.shape[1])
+    stored, sketch = finish(incoming, probe, slot_table)
     return (stored, sketch)
 
 

time: 102 us -> 93.9 us (0.921)
  Pallas kernels: 97.1 us -> 93 us
  other arithmetic: 3.5 us -> 0 us
    pallas_call x1, Pallas kernels: 11.4 us -> 7.2 us  [finish(): pl.pallas_call(finish_kernel, grid_spec=pltpu.PrefetchScalarGridSpec(num_...]
    select_n x2 -> x0, other arithmetic: 2.01 us -> none  [the longest x1 1.3 us: shards(): source = mine % total_blocks // per_rank]
where the time goes in v4:
time: 93.9 us; the launch traced here: 93.7 us
  Pallas kernels  93 us (99%)
    pallas_call x1, Pallas kernels, save(): pl.pallas_call(save_kernel, grid_spec=pltpu.PrefetchScalarGridSpec(num_sc...  85.8 us
    pallas_call x1, Pallas kernels, finish(): pl.pallas_call(finish_kernel, grid_spec=pltpu.PrefetchScalarGridSpec(num_...  7.2 us

profile of v4, /device:TPU:1, one launch (start us, length us, event | category | flops | bytes accessed | tf_op | source)
XLA Modules:
  0.0 93.7 jit_solution(11594928172069763345)
XLA Ops:
  0.6 0.0 copy-start
  0.6 85.8 %shard_map.68 = bf16[128,128,128]{2,1,0:T(8,128)(2,1)S(1)} custom-call(s32[2,17]{1,0:T(2,128)} %offsets.1, s32[2048]{0:T(1024)} %table.3, bf16[12288,128]{1,0:T(8,128)(2,1)} %embed.1, bf16[12288,128]{1,0:T(8,128)(2,1)} %head.1), custom_call_target="tpu_custom_call" | custom-call | tf_op jit(solution)/shard_map/pallas_call | solution.py:223
  86.5 0.0 copy-done
  86.5 7.2 %shard_map.69 = (bf16[16,128,1024]{2,1,0:T(8,128)(2,1)}, f32[2048,1024]{1,0:T(8,128)}) custom-call(s32[2048]{0:T(1024)} %table.3, bf16[8,16,128,128]{3,2,1,0:T(8,128)(2,1)S(1)} %bitcast.2, bf16[1024,1024]{1,0:T(8,128)(2,1)S(1)} %copy-done), custom_call_target="tpu_custom_call" | custom-call | tf_op jit(solution)/shard_map/pallas_call | solution.py:300
Async XLA Ops:
  0.6 85.8 %copy-start = (bf16[1024,1024]{1,0:T(8,128)(2,1)S(1)}, bf16[1024,1024]{1,0:T(8,128)(2,1)}, u32[]{:S(2)}) copy-start(bf16[1024,1024]{1,0:T(8,128)(2,1)} %weights.1) | copy-start | bytes 6291460

commit v5 on v4

v5 whole, which is shorter than its diff:
```python
import functools
import itertools
import random

import jax
import jax.numpy as jnp
from jax import lax
from jax.experimental import pallas as pl
from jax.experimental.pallas import tpu as pltpu
from jax.sharding import PartitionSpec as P

R = 8192
BLOCK = 128
MESH = pl.DeviceIdType.MESH
Z = 4
Y = 4
X = 4
QUARTER = R // 4
LIFT = 16
TRAIL = QUARTER + LIFT
HIGH = R - QUARTER
PAD = BLOCK
OWN = PAD + R + QUARTER
FOREIGN = PAD + TRAIL
STEP = 3 * LIFT
UNROLL = 4
PIECES = ((0, 0, TRAIL), (1, 0, 32 * STEP), (1, 32 * STEP, 11 * STEP))
ROUNDS = (0, 4, 8) + tuple(range(16, 129, 8))


def exchange_order():
    offsets = list(itertools.product(range(Z), range(2), range(Y), range(X)))[1:]
    random.Random(0).shuffle(offsets)
    offsets.sort(key=lambda o: -sum(min(a, 4 - a) for a in (o[0], o[2], o[3])))
    return offsets + [(0, 0, 0, 0)]


ORDER = exchange_order()


def save_kernel(
    offsets_hbm, table_hbm, embed, head, gathered, offsets, table, incoming, lookup, picked, low, high, own, arrived, foreign, trail, packed,
    load_sem, shift_send, shift_recv, scalar_sem, send_sem, recv_sem, plane_sem, space_sem,
):
    data = lax.axis_index("dp")
    tensor = lax.axis_index("tensor")
    me = data * (Y * X) + tensor
    z, core, y, x = data // 2, data % 2, tensor // X, tensor % X
    ranks = Y * X
    following = (data, (tensor + 1) % ranks)
    previous = (data, (tensor + ranks - 1) % ranks)

    def peer(offset):
        dz, dc, dy, dx = offset
        return (((z + dz) % Z) * 2 + (core + dc) % 2, ((y + dy) % Y) * X + (x + dx) % X)

    def signal(sem, device):
        pl.semaphore_signal(sem, inc=1, device_id=device, device_id_type=MESH)

    sources = (embed, head)
    height = embed.shape[0]

    def load(m, part):
        if part == 0:
            return pltpu.make_async_copy(
                sources[m].at[pl.ds(HIGH, height - HIGH)],
                high.at[pl.ds(m * (height - HIGH), height - HIGH)],
                load_sem.at[0, m],
            )
        return pltpu.make_async_copy(sources[m].at[pl.ds(0, HIGH)], low.at[m], load_sem.at[1, m])

    row = [(0, dc, 0, dx) for dc in range(2) for dx in range(X) if (dc, dx) != (0, 0)]
    column = [(0, 0, d, 0) for d in range(1, Y)]
    stack = [(d, 0, 0, 0) for d in range(1, Z)]
    barrier = pltpu.get_barrier_semaphore()
    signal(barrier, following)
    signal(barrier, previous)
    for offset in stack + column + row:
        signal(barrier, peer(offset))
    scalars = [
        pltpu.make_async_copy(offsets_hbm, offsets, scalar_sem.at[0]),
        pltpu.make_async_copy(table_hbm, table, scalar_sem.at[1]),
    ]
    for copy in scalars:
        copy.start()
    for part in range(2):
        for m in range(2):
            load(m, part).start()
    pl.semaphore_wait(barrier, 2 + len(stack + column + row))

    def shift(side, piece):
        m, first, rows = PIECES[piece]
        if side == 0:
            source = trail.at[m, pl.ds(first, rows)]
        else:
            rows = min(rows, QUARTER - first)
            source = sources[m].at[pl.ds(first, rows)]
        return pltpu.make_async_remote_copy(
            src_ref=source,
            dst_ref=arrived.at[m, side, pl.ds(first, rows)],
            send_sem=shift_send.at[side, piece],
            recv_sem=shift_recv.at[side, piece],
            device_id=(following, previous)[side],
            device_id_type=MESH,
        )

    for piece in range(len(PIECES)):
        shift(1, piece).start()
    for copy in scalars:
        copy.wait()
    load(0, 0).wait()
    load(1, 0).wait()
    for m in range(2):
        begin = (tensor + 1) * R - offsets[m, tensor] - HIGH
        begin = jnp.clip(begin, 0, height - HIGH - TRAIL + LIFT - 1)
        begin = lax.div(begin, LIFT) * LIFT
        begin = m * (height - HIGH) + begin
        trail[m] = high[pl.ds(begin, TRAIL), :]
    for piece in range(len(PIECES)):
        shift(0, piece).start()

    for offset in column:
        signal(plane_sem, peer(offset))
    pl.semaphore_wait(plane_sem, len(column))
    for offset in stack:
        signal(space_sem, peer(offset))
    per_rank = R // BLOCK
    slots = table.shape[0] // len(ORDER)

    @pl.loop(0, len(ORDER))
    def _(j):
        total = jnp.int32(0)
        for s in range(slots):
            number = table[j * slots + s]
            half = lax.div(number, per_rank * ranks)
            block = lax.rem(number, per_rank)
            rank = lax.rem(lax.div(number, per_rank), ranks)
            other = jnp.minimum(jnp.abs(rank - tensor), 1)
            total += (half * per_rank + block) * (1 - other)
        picked[j] = jnp.clip(total, 0, 2 * per_rank - 1)

    for k, offset in enumerate(ORDER):
        to = peer(offset)
        lookup[k] = to[0] * ranks + to[1]

    load(0, 1).wait()
    load(1, 1).wait()
    step = 256
    for m in range(2):

        @pl.loop(0, HIGH // step)
        def _(i):
            at = pl.multiple_of(i * step, step)
            own[pl.ds(m * OWN + PAD + at, step), :] = low[m, pl.ds(at, step), :].astype(jnp.float32)

        @pl.loop(0, (R + QUARTER - HIGH) // step)
        def _(i):
            at = pl.multiple_of(i * step, step)
            rows = high[pl.ds(m * (height - HIGH) + at, step), :]
            own[pl.ds(m * OWN + PAD + HIGH + at, step), :] = rows.astype(jnp.float32)

    pl.semaphore_wait(space_sem, len(stack))

    for piece, (m, first_row, rows) in enumerate(PIECES):
        for side in range(2):
            shift(side, piece).wait_recv()

            @pl.loop(0, rows // STEP)
            def _(i):
                at = pl.multiple_of(first_row + i * STEP, LIFT)
                rows = arrived[m, side, pl.ds(at, STEP), :].astype(jnp.float32)
                foreign[pl.ds((m * 2 + side) * FOREIGN + PAD + at, STEP), :] = rows

    earlier = (tensor + ranks - 1) % ranks
    befores = [offsets[m, tensor] - tensor * R for m in range(2)]
    afters = [offsets[m, tensor + 1] - tensor * R for m in range(2)]
    lifts = [lax.rem((earlier + 1) * R - offsets[m, earlier], LIFT) for m in range(2)]
    local_row = lax.broadcasted_iota(jnp.int32, (BLOCK, embed.shape[1]), 0)

    def pack(k):
        local = picked[lookup[k]]
        m = lax.div(local, per_rank)
        block = lax.rem(local, per_rank)
        first = block * BLOCK
        before = befores[0] + m * (befores[1] - befores[0])
        after = afters[0] + m * (afters[1] - afters[0])
        lift = lifts[0] + m * (lifts[1] - lifts[0])
        own_at = m * OWN + PAD + jnp.clip(first - before, -PAD, R + QUARTER - BLOCK)
        left_at = jnp.clip(first + lift, -PAD, TRAIL - BLOCK)
        right_at = jnp.clip(first - after, -PAD, TRAIL - BLOCK)
        side = lax.div(block, per_rank // 2)
        at = (m * 2 + side) * FOREIGN + PAD + left_at + side * (right_at - left_at)
        mine = own[pl.ds(own_at, BLOCK), :]
        theirs = foreign[pl.ds(at, BLOCK), :]
        keep = (local_row >= before - first) & (local_row < after - first)
        packed[k] = jnp.where(keep, mine, theirs).astype(packed.dtype)

    def send(k):
        return pltpu.make_async_remote_copy(
            src_ref=packed.at[k],
            dst_ref=incoming.at[me],
            send_sem=send_sem,
            recv_sem=recv_sem,
            device_id=peer(ORDER[k]),
            device_id_type=MESH,
        )

    count = len(ORDER)
    for start, stop, behind in zip(ROUNDS, ROUNDS[1:] + (count,), (0,) + ROUNDS):
        if start < stop:

            @pl.loop(start, stop, unroll=UNROLL)
            def _(k):
                pack(k)

        for k in range(behind, min(start, count - 1)):
            send(k).start()
    incoming[me] = packed[count - 1]
    everything = packed.at[pl.ds(0, count - 1)]
    pltpu.make_async_copy(everything, everything, recv_sem).wait()
    width = embed.shape[1]

    @pl.loop(0, slots, unroll=2)
    def _(slot):
        rank = lax.rem(lax.div(table[me * slots + slot], per_rank), ranks)
        at = pl.ds(pl.multiple_of(slot * BLOCK, BLOCK), BLOCK)
        for d in range(2 * Z):
            gathered[at, d * width:(d + 1) * width] = incoming[d * ranks + rank]

    pltpu.make_async_copy(everything, everything, send_sem).wait()
    for piece in range(len(PIECES)):
        for side in range(2):
            shift(side, piece).wait_send()


def save(embed_rows, head_rows, row_offsets, slot_table):
    height, width = embed_rows.shape
    dtype = embed_rows.dtype
    slots = slot_table.shape[0] // len(ORDER)
    return pl.pallas_call(
        save_kernel,
        in_specs=[pl.BlockSpec(memory_space=pl.ANY)] * 4,
        out_specs=pl.BlockSpec(memory_space=pltpu.VMEM),
        scratch_shapes=[
            pltpu.SMEM(row_offsets.shape, jnp.int32),
            pltpu.SMEM(slot_table.shape, jnp.int32),
            pltpu.VMEM((len(ORDER), BLOCK, width), dtype),
            pltpu.SMEM((len(ORDER),), jnp.int32),
            pltpu.SMEM((len(ORDER),), jnp.int32),
            pltpu.VMEM((2, HIGH, width), dtype),
            pltpu.VMEM((2 * (height - HIGH), width), dtype),
            pltpu.VMEM((2 * OWN, width), jnp.float32),
            pltpu.VMEM((2, 2, TRAIL, width), dtype),
            pltpu.VMEM((4 * FOREIGN, width), jnp.float32),
            pltpu.VMEM((2, TRAIL, width), dtype),
            pltpu.VMEM((len(ORDER), BLOCK, width), dtype),
            pltpu.SemaphoreType.DMA((2, 2)),
            pltpu.SemaphoreType.DMA((2, len(PIECES))),
            pltpu.SemaphoreType.DMA((2, len(PIECES))),
            pltpu.SemaphoreType.DMA((2,)),
            pltpu.SemaphoreType.DMA,
            pltpu.SemaphoreType.DMA,
            pltpu.SemaphoreType.REGULAR,
            pltpu.SemaphoreType.REGULAR,
        ],
        out_shape=pltpu.VMEM((slots * BLOCK, 2 * Z * width), dtype),
        compiler_params=pltpu.CompilerParams(
            collective_id=0, has_side_effects=True, vmem_limit_bytes=38 << 20
        ),
    )(row_offsets, slot_table, embed_rows, head_rows)


ROWS = 256
BUFFERS = 4


def finish_kernel(gathered, weights, stored, sketch, product, stored_sem, sketch_sem):
    groups = gathered.shape[0] // ROWS

    def put_stored(g):
        at = pl.ds(g * ROWS, ROWS)
        return pltpu.make_async_copy(gathered.at[at], stored.at[at], stored_sem.at[g])

    def put_sketch(g):
        return pltpu.make_async_copy(
            product.at[g % BUFFERS], sketch.at[pl.ds(g * ROWS, ROWS)], sketch_sem.at[g]
        )

    for g in range(groups):
        put_stored(g).start()
    for g in range(groups):
        if g >= BUFFERS:
            put_sketch(g - BUFFERS).wait()
        x = gathered[g * ROWS:(g + 1) * ROWS]
        product[g % BUFFERS] = jnp.dot(x, weights[...], preferred_element_type=jnp.float32)
        put_sketch(g).start()
    for g in range(groups):
        put_stored(g).wait()
    for g in range(groups - BUFFERS, groups):
        put_sketch(g).wait()


def finish(gathered, probe):
    rows, columns = gathered.shape
    return pl.pallas_call(
        finish_kernel,
        in_specs=[pl.BlockSpec(memory_space=pltpu.VMEM)] * 2,
        out_specs=[pl.BlockSpec(memory_space=pl.ANY)] * 2,
        scratch_shapes=[
            pltpu.VMEM((BUFFERS, ROWS, probe.shape[1]), jnp.float32),
            pltpu.SemaphoreType.DMA((rows // ROWS,)),
            pltpu.SemaphoreType.DMA((rows // ROWS,)),
        ],
        out_shape=[
            jax.ShapeDtypeStruct((rows, columns), gathered.dtype),
            jax.ShapeDtypeStruct((rows, probe.shape[1]), jnp.float32),
        ],
        compiler_params=pltpu.CompilerParams(vmem_limit_bytes=20 << 20),
    )(gathered, probe)


def shards(embed_rows, head_rows, row_offsets, slot_table, probe):
    probe = pltpu.with_memory_space_constraint(probe, pltpu.VMEM)
    embed_rows, head_rows, row_offsets, slot_table = (
        pltpu.with_memory_space_constraint(a, pltpu.HBM)
        for a in (embed_rows, head_rows, row_offsets, slot_table)
    )
    gathered = save(embed_rows, head_rows, row_offsets, slot_table)
    stored, sketch = finish(gathered, probe)
    return (stored.reshape(-1, BLOCK, stored.shape[1]), sketch.reshape(-1, BLOCK, sketch.shape[1]))


def solution(mesh):
    return jax.shard_map(
        shards,
        mesh=mesh,
        in_specs=(P("tensor", "dp"), P("tensor", "dp"), P(), P(), P()),
        out_specs=(P(("dp", "tensor"), None, None), P(("dp", "tensor"), None, None)),
        check_vma=False,
    )
```

time: 93.9 us -> 91.6 us (0.976)
  Pallas kernels: 93 us -> 90.4 us
    pallas_call x2, Pallas kernels: 93 us -> 90.4 us  [the longest x1 84.1 us: save(): pl.pallas_call(save_kernel, in_specs=[pl.BlockSpec(memory_space=pl.ANY)]...]
where the time goes in v5:
time: 91.6 us; the launch traced here: 91 us
  Pallas kernels  90.4 us (99%)
    pallas_call x1, Pallas kernels, save(): pl.pallas_call(save_kernel, in_specs=[pl.BlockSpec(memory_space=pl.ANY)]...  84.1 us
    pallas_call x1, Pallas kernels, finish(): pl.pallas_call(finish_kernel, in_specs=[pl.BlockSpec(memory_space=pltpu.V...  6.31 us

profile of v5, /device:TPU:1, one launch (start us, length us, event | category | flops | bytes accessed | tf_op | source)
XLA Modules:
  0.0 91.0 jit_solution(11770159874125446202)
XLA Ops:
  0.6 0.0 copy-start
  0.6 84.1 %shard_map.68.gathered = bf16[2048,1024]{1,0:T(8,128)(2,1)S(1)} custom-call(s32[2,17]{1,0:T(2,128)} %offsets_hbm.1, s32[2048]{0:T(1024)} %table_hbm.1, bf16[12288,128]{1,0:T(8,128)(2,1)} %embed.1, bf16[12288,128]{1,0:T(8,128)(2,1)} %head.1), custom_call_target="tpu_custom_call" | custom-call | tf_op jit(solution)/shard_map/pallas_call | solution.py:240
  84.7 0.0 copy-done
  84.7 6.3 %shard_map.69 = (bf16[2048,1024]{1,0:T(8,128)(2,1)}, f32[2048,1024]{1,0:T(8,128)}) custom-call(bf16[2048,1024]{1,0:T(8,128)(2,1)S(1)} %shard_map.68.gathered, bf16[1024,1024]{1,0:T(8,128)(2,1)S(1)} %copy-done), custom_call_target="tpu_custom_call" | custom-call | tf_op jit(solution)/shard_map/pallas_call | solution.py:305
Async XLA Ops:
  0.6 84.1 %copy-start = (bf16[1024,1024]{1,0:T(8,128)(2,1)S(1)}, bf16[1024,1024]{1,0:T(8,128)(2,1)}, u32[]{:S(2)}) copy-start(bf16[1024,1024]{1,0:T(8,128)(2,1)} %weights.1) | copy-start | bytes 6291460

commit v6 on v5

--- a/solution.py
+++ b/solution.py
@@ -39,7 +39,7 @@
 
 
 def save_kernel(
-    offsets_hbm, table_hbm, embed, head, gathered, offsets, table, incoming, lookup, picked, low, high, own, arrived, foreign, trail, packed,
+    offsets_hbm, table_hbm, embed, head, gathered, offsets, table, incoming, lookup, picked, low, high_embed, high_head, own, arrived, foreign, trail, packed,
     load_sem, shift_send, shift_recv, scalar_sem, send_sem, recv_sem, plane_sem, space_sem,
 ):
     data = lax.axis_index("dp")
@@ -58,13 +58,14 @@
         pl.semaphore_signal(sem, inc=1, device_id=device, device_id_type=MESH)
 
     sources = (embed, head)
+    high = (high_embed, high_head)
     height = embed.shape[0]
 
     def load(m, part):
         if part == 0:
             return pltpu.make_async_copy(
                 sources[m].at[pl.ds(HIGH, height - HIGH)],
-                high.at[pl.ds(m * (height - HIGH), height - HIGH)],
+                high[m],
                 load_sem.at[0, m],
             )
         return pltpu.make_async_copy(sources[m].at[pl.ds(0, HIGH)], low.at[m], load_sem.at[1, m])
@@ -83,9 +84,8 @@
     ]
     for copy in scalars:
         copy.start()
-    for part in range(2):
-        for m in range(2):
-            load(m, part).start()
+    load(0, 0).start()
+    load(1, 0).start()
     pl.semaphore_wait(barrier, 2 + len(stack + column + row))
 
     def shift(side, piece):
@@ -106,18 +106,18 @@
 
     for piece in range(len(PIECES)):
         shift(1, piece).start()
-    for copy in scalars:
-        copy.wait()
-    load(0, 0).wait()
-    load(1, 0).wait()
+    scalars[0].wait()
     for m in range(2):
+        load(m, 0).wait()
         begin = (tensor + 1) * R - offsets[m, tensor] - HIGH
         begin = jnp.clip(begin, 0, height - HIGH - TRAIL + LIFT - 1)
         begin = lax.div(begin, LIFT) * LIFT
-        begin = m * (height - HIGH) + begin
-        trail[m] = high[pl.ds(begin, TRAIL), :]
-    for piece in range(len(PIECES)):
-        shift(0, piece).start()
+        trail[m] = high[m][pl.ds(begin, TRAIL), :]
+        load(m, 1).start()
+        for piece in range(len(PIECES)):
+            if PIECES[piece][0] == m:
+                shift(0, piece).start()
+    scalars[1].wait()
 
     for offset in column:
         signal(plane_sem, peer(offset))
@@ -156,7 +156,7 @@
         @pl.loop(0, (R + QUARTER - HIGH) // step)
         def _(i):
             at = pl.multiple_of(i * step, step)
-            rows = high[pl.ds(m * (height - HIGH) + at, step), :]
+            rows = high[m][pl.ds(at, step), :]
             own[pl.ds(m * OWN + PAD + HIGH + at, step), :] = rows.astype(jnp.float32)
 
     pl.semaphore_wait(space_sem, len(stack))
@@ -248,7 +248,8 @@
             pltpu.SMEM((len(ORDER),), jnp.int32),
             pltpu.SMEM((len(ORDER),), jnp.int32),
             pltpu.VMEM((2, HIGH, width), dtype),
-            pltpu.VMEM((2 * (height - HIGH), width), dtype),
+            pltpu.VMEM((height - HIGH, width), dtype),
+            pltpu.VMEM((height - HIGH, width), dtype),
             pltpu.VMEM((2 * OWN, width), jnp.float32),
             pltpu.VMEM((2, 2, TRAIL, width), dtype),
             pltpu.VMEM((4 * FOREIGN, width), jnp.float32),

time: 91.6 us -> 92.1 us (level)
  no operation moved by 1% of the time
where the time goes in v6:
time: 92.1 us; the launch traced here: 90.8 us
  Pallas kernels  90.1 us (98%)
    pallas_call x1, Pallas kernels, save(): pl.pallas_call(save_kernel, in_specs=[pl.BlockSpec(memory_space=pl.ANY)]...  83.8 us
    pallas_call x1, Pallas kernels, finish(): pl.pallas_call(finish_kernel, in_specs=[pl.BlockSpec(memory_space=pltpu.V...  6.3 us

profile of v6, /device:TPU:1, one launch (start us, length us, event | category | flops | bytes accessed | tf_op | source)
XLA Modules:
  0.0 90.8 jit_solution(9515023900473050556)
XLA Ops:
  0.6 0.0 copy-start
  0.6 83.8 %shard_map.68.gathered = bf16[2048,1024]{1,0:T(8,128)(2,1)S(1)} custom-call(s32[2,17]{1,0:T(2,128)} %offsets_hbm.1, s32[2048]{0:T(1024)} %table_hbm.1, bf16[12288,128]{1,0:T(8,128)(2,1)} %embed.1, bf16[12288,128]{1,0:T(8,128)(2,1)} %head.1), custom_call_target="tpu_custom_call" | custom-call | tf_op jit(solution)/shard_map/pallas_call | solution.py:240
  84.5 0.0 copy-done
  84.5 6.3 %shard_map.69 = (bf16[2048,1024]{1,0:T(8,128)(2,1)}, f32[2048,1024]{1,0:T(8,128)}) custom-call(bf16[2048,1024]{1,0:T(8,128)(2,1)S(1)} %shard_map.68.gathered, bf16[1024,1024]{1,0:T(8,128)(2,1)S(1)} %copy-done), custom_call_target="tpu_custom_call" | custom-call | tf_op jit(solution)/shard_map/pallas_call | solution.py:306
Async XLA Ops:
  0.6 83.8 %copy-start = (bf16[1024,1024]{1,0:T(8,128)(2,1)S(1)}, bf16[1024,1024]{1,0:T(8,128)(2,1)}, u32[]{:S(2)}) copy-start(bf16[1024,1024]{1,0:T(8,128)(2,1)} %weights.1) | copy-start | bytes 6291460

commit v7 on v6

--- a/solution.py
+++ b/solution.py
@@ -30,7 +30,7 @@
 
 def exchange_order():
     offsets = list(itertools.product(range(Z), range(2), range(Y), range(X)))[1:]
-    random.Random(0).shuffle(offsets)
+    random.Random(1).shuffle(offsets)
     offsets.sort(key=lambda o: -sum(min(a, 4 - a) for a in (o[0], o[2], o[3])))
     return offsets + [(0, 0, 0, 0)]
 

time: 92.1 us -> 90.1 us (0.978); the launches traced: 90.8 us -> 90 us
  no operation moved by 1% of the time
where the time goes in v7:
time: 90.1 us; the launch traced here: 90 us
  Pallas kernels  89.3 us (99%)
    pallas_call x1, Pallas kernels, save(): pl.pallas_call(save_kernel, in_specs=[pl.BlockSpec(memory_space=pl.ANY)]...  83 us
    pallas_call x1, Pallas kernels, finish(): pl.pallas_call(finish_kernel, in_specs=[pl.BlockSpec(memory_space=pltpu.V...  6.31 us

profile of v7, /device:TPU:1, one launch (start us, length us, event | category | flops | bytes accessed | tf_op | source)
XLA Modules:
  0.0 90.0 jit_solution(9968317701447128529)
XLA Ops:
  0.6 0.0 copy-start
  0.6 83.0 %shard_map.68.gathered = bf16[2048,1024]{1,0:T(8,128)(2,1)S(1)} custom-call(s32[2,17]{1,0:T(2,128)} %offsets_hbm.1, s32[2048]{0:T(1024)} %table_hbm.1, bf16[12288,128]{1,0:T(8,128)(2,1)} %embed.1, bf16[12288,128]{1,0:T(8,128)(2,1)} %head.1), custom_call_target="tpu_custom_call" | custom-call | tf_op jit(solution)/shard_map/pallas_call | solution.py:240
  83.6 0.0 copy-done
  83.7 6.3 %shard_map.69 = (bf16[2048,1024]{1,0:T(8,128)(2,1)}, f32[2048,1024]{1,0:T(8,128)}) custom-call(bf16[2048,1024]{1,0:T(8,128)(2,1)S(1)} %shard_map.68.gathered, bf16[1024,1024]{1,0:T(8,128)(2,1)S(1)} %copy-done), custom_call_target="tpu_custom_call" | custom-call | tf_op jit(solution)/shard_map/pallas_call | solution.py:306
Async XLA Ops:
  0.6 83.0 %copy-start = (bf16[1024,1024]{1,0:T(8,128)(2,1)S(1)}, bf16[1024,1024]{1,0:T(8,128)(2,1)}, u32[]{:S(2)}) copy-start(bf16[1024,1024]{1,0:T(8,128)(2,1)} %weights.1) | copy-start | bytes 6291460

commit v8 on v7

--- a/solution.py
+++ b/solution.py
@@ -54,6 +54,11 @@
         dz, dc, dy, dx = offset
         return (((z + dz) % Z) * 2 + (core + dc) % 2, ((y + dy) % Y) * X + (x + dx) % X)
 
+    def target(offset):
+        dz, dc, dy, dx = offset
+        dz, dy, dx = (dz + core * (dy - dz), dy + core * (dx - dy), dx + core * (dz - dx))
+        return (((z + dz) % Z) * 2 + (core + dc) % 2, ((y + dy) % Y) * X + (x + dx) % X)
+
     def signal(sem, device):
         pl.semaphore_signal(sem, inc=1, device_id=device, device_id_type=MESH)
 
@@ -140,7 +145,7 @@
         picked[j] = jnp.clip(total, 0, 2 * per_rank - 1)
 
     for k, offset in enumerate(ORDER):
-        to = peer(offset)
+        to = target(offset)
         lookup[k] = to[0] * ranks + to[1]
 
     load(0, 1).wait()
@@ -201,7 +206,7 @@
             dst_ref=incoming.at[me],
             send_sem=send_sem,
             recv_sem=recv_sem,
-            device_id=peer(ORDER[k]),
+            device_id=target(ORDER[k]),
             device_id_type=MESH,
         )
 

time: 90.1 us -> 90 us (level)
  no operation moved by 1% of the time
where the time goes in v8:
time: 90 us; the launch traced here: 89.9 us
  Pallas kernels  89.2 us (99%)
    pallas_call x1, Pallas kernels, save(): pl.pallas_call(save_kernel, in_specs=[pl.BlockSpec(memory_space=pl.ANY)]...  82.9 us
    pallas_call x1, Pallas kernels, finish(): pl.pallas_call(finish_kernel, in_specs=[pl.BlockSpec(memory_space=pltpu.V...  6.31 us

profile of v8, /device:TPU:1, one launch (start us, length us, event | category | flops | bytes accessed | tf_op | source)
XLA Modules:
  0.0 89.9 jit_solution(9948352479192917876)
XLA Ops:
  0.6 0.0 copy-start
  0.6 82.9 %shard_map.68.gathered = bf16[2048,1024]{1,0:T(8,128)(2,1)S(1)} custom-call(s32[2,17]{1,0:T(2,128)} %offsets_hbm.1, s32[2048]{0:T(1024)} %table_hbm.1, bf16[12288,128]{1,0:T(8,128)(2,1)} %embed.1, bf16[12288,128]{1,0:T(8,128)(2,1)} %head.1), custom_call_target="tpu_custom_call" | custom-call | tf_op jit(solution)/shard_map/pallas_call | solution.py:245
  83.5 0.0 copy-done
  83.6 6.3 %shard_map.69 = (bf16[2048,1024]{1,0:T(8,128)(2,1)}, f32[2048,1024]{1,0:T(8,128)}) custom-call(bf16[2048,1024]{1,0:T(8,128)(2,1)S(1)} %shard_map.68.gathered, bf16[1024,1024]{1,0:T(8,128)(2,1)S(1)} %copy-done), custom_call_target="tpu_custom_call" | custom-call | tf_op jit(solution)/shard_map/pallas_call | solution.py:311
Async XLA Ops:
  0.6 82.9 %copy-start = (bf16[1024,1024]{1,0:T(8,128)(2,1)S(1)}, bf16[1024,1024]{1,0:T(8,128)(2,1)}, u32[]{:S(2)}) copy-start(bf16[1024,1024]{1,0:T(8,128)(2,1)} %weights.1) | copy-start | bytes 6291460
